TPU v7x, 32 devices: a whole 2x2x4 slice. The times are simulated.
32 devices in a mesh: gx: 2 (over x), gy: 4 (over z), gz: 4 (over y, core).
Axes of the slice: x: 2, y: 2, z: 4, core: 2. Of those that a mesh axis runs over, the one named last changes fastest.
Arguments:
- density: float32 [32, 64, 512], P('gx', 'gy', 'gz'), may hold values from 0.005 to 0.6, as said below
- coupling: float32 [14, 14], replicated, may hold values from -0.3 to 1.5, as said below
Outputs:
- potentials: float32 [14, 32, 64, 512], P(None, 'gx', 'gy', 'gz')
Inputs may be any that keep to these rules, and one draw needn't show every extreme that they name: Positive density. `coupling`: symmetric.
All inputs are finite; a program needn't handle non-finite values.
Results may differ from a plain program's by a relative error of at most 0.0003.
Values sent between devices are 32-bit elements; how exact they have to be, the bound alone decides.
A program may use at most 128 MiB of HBM per device.

v0:
```python
import math

import jax
import jax.numpy as jnp
from jax import lax
from jax.sharding import PartitionSpec as P

zab_ratio = 0.8491 / 9.0
q_cut = 5.0
mesh_step = 0.07
range_factor = 1.0
local_weight = 0.25
spline_root = math.sqrt(3.0) - 2.0
highest = lax.Precision.HIGHEST


def extended(cells, sides, width):
    for axis, dim in sides:
        count = lax.axis_size(axis)
        head = lax.slice_in_dim(cells, 0, width, axis=dim)
        tail = lax.slice_in_dim(cells, cells.shape[dim] - width, cells.shape[dim], axis=dim)
        cells = jnp.concatenate(
            [
                lax.ppermute(tail, axis, [(i, (i + 1) % count) for i in range(count)]),
                cells,
                lax.ppermute(head, axis, [((i + 1) % count, i) for i in range(count)]),
            ],
            axis=dim,
        )
    return cells


def interior(padded, dim_index, offset):
    picks = []
    for other in range(3):
        lowest = 2 + offset if other == dim_index else 2
        picks.append(slice(lowest, lowest + padded.shape[other] - 4))
    return padded[tuple(picks)]


def saturated_wavevector(density, grad_sq):
    fermi_k = jnp.cbrt(3.0 * math.pi * math.pi * density)
    reduced = grad_sq / (4.0 * fermi_k * fermi_k * density * density)
    raw_q = fermi_k * (1.0 + zab_ratio * reduced)
    scaled = raw_q / q_cut
    powered = scaled
    series = jnp.zeros_like(scaled)
    for term_order in range(1, 13):
        series = series + powered / term_order
        powered = powered * scaled
    return q_cut * (1.0 - jnp.exp(-series))


def spline_weights(q_zero, q_top, qpoints):
    position = jnp.maximum(qpoints - 1.0 + jnp.log(q_zero / q_top) / mesh_step, 0.0)
    knot_ids = jnp.arange(-1, qpoints + 1, dtype=jnp.int32)
    offset = jnp.abs(position[None, :] - knot_ids.astype(jnp.float32)[:, None])
    bspline = (
        jnp.maximum(2.0 - offset, 0.0) ** 3 - 4.0 * jnp.maximum(1.0 - offset, 0.0) ** 3
    ) / 6.0
    q_nodes = jnp.arange(qpoints, dtype=jnp.int32)
    distance = jnp.abs(knot_ids[:, None] - q_nodes[None, :])
    parity = (1 - 2 * (distance % 2)).astype(jnp.float32)
    matrix = (
        math.sqrt(3.0) * parity * jnp.exp(distance.astype(jnp.float32) * math.log(-spline_root))
    )
    return jnp.dot(matrix.T, bspline, precision=highest)


def build_thetas(dens_field, q_field, q_top, qpoints):
    weights = spline_weights(q_field.reshape(-1), q_top, qpoints)
    return (weights * dens_field.reshape(1, -1)).reshape((qpoints,) + dens_field.shape)


def join_planes(joined, count, slab_rows, groups_y, groups_z):
    size_y, size_z = (joined.shape[-2], joined.shape[-1])
    planes = joined.reshape(count, slab_rows, groups_y, groups_z, size_y, size_z)
    return planes.transpose(0, 1, 2, 4, 3, 5).reshape(
        count, slab_rows, groups_y * size_y, groups_z * size_z
    )


def wave_squared(wave_ids, length):
    folded = jnp.where(2 * wave_ids < length, wave_ids, wave_ids - length)
    wavenum = 2.0 * math.pi / length * folded.astype(jnp.float32)
    return wavenum * wavenum


def dft_tables(length):
    wave_ids = jnp.arange(length, dtype=jnp.int32)
    phases = wave_ids[:, None] * wave_ids[None, :] % length
    angles = 2.0 * math.pi / length * phases.astype(jnp.float32)
    return (jnp.cos(angles), jnp.sin(angles))


def complex_table(length, direction_sign):
    cosine, sines = dft_tables(length)
    top_row = jnp.stack([cosine, -direction_sign * sines], axis=1)
    bottom_row = jnp.stack([direction_sign * sines, cosine], axis=1)
    return jnp.stack([top_row, bottom_row], axis=0)


def forward_z(field_in):
    cosine, sines = dft_tables(field_in.shape[-1])
    matrix = jnp.stack([cosine, -sines], axis=1)
    return jnp.einsum("aryz,zpk->paryk", field_in, matrix, precision=highest)


def along_y(complex_pair, direction_sign):
    matrix = complex_table(complex_pair.shape[3], direction_sign)
    return jnp.einsum("pkqy,qaryz->parkz", matrix, complex_pair, precision=highest)


def along_x(complex_pair, direction_sign):
    matrix = complex_table(complex_pair.shape[2], direction_sign)
    return jnp.einsum("pkqx,qaxm->pakm", matrix, complex_pair, precision=highest)


def inverse_z(complex_pair):
    cosine, sines = dft_tables(complex_pair.shape[-1])
    matrix = jnp.stack([cosine, -sines], axis=0)
    return jnp.einsum("paryz,pzk->aryk", complex_pair, matrix, precision=highest)


def apply_kernel(spectra, k_squared, coupling, q_top):
    qpoints = coupling.shape[0]
    q_nodes = jnp.arange(qpoints, dtype=jnp.int32)
    q_mesh = q_top * jnp.exp(-mesh_step * (qpoints - 1 - q_nodes).astype(jnp.float32))
    masses = range_factor * q_mesh[:, None] * q_mesh[None, :]

    def add_source(source, summed):
        mass_col = lax.dynamic_index_in_dim(masses, source, 1, keepdims=False)[:, None, None]
        coupling_col = lax.dynamic_index_in_dim(coupling, source, 1, keepdims=False)[:, None, None]
        factor = coupling_col * (local_weight + mass_col / (k_squared[None] + mass_col))
        spectrum = lax.dynamic_index_in_dim(spectra, source, 1, keepdims=False)
        return summed + factor[None] * spectrum[:, None]

    return lax.fori_loop(0, qpoints, add_source, jnp.zeros_like(spectra))


def body(density, coupling):
    size_x, size_y, size_z = density.shape
    qpoints = coupling.shape[0]
    groups_x, groups_y, groups_z = (lax.axis_size("gx"), lax.axis_size("gy"), lax.axis_size("gz"))
    full_x, full_y, full_z = (size_x * groups_x, size_y * groups_y, size_z * groups_z)
    scale_inv = 1.0 / (full_x * full_y * full_z)
    padded = extended(density, (("gx", 0), ("gy", 1), ("gz", 2)), 2)
    grad_sq = jnp.zeros_like(density)
    for dim_index in range(3):
        nearer = interior(padded, dim_index, 1) - interior(padded, dim_index, -1)
        farther = interior(padded, dim_index, 2) - interior(padded, dim_index, -2)
        gradient = (8.0 * nearer - farther) / 12.0
        grad_sq = grad_sq + gradient * gradient
    q_zero = saturated_wavevector(density, grad_sq)
    q_top = lax.pmax(jnp.max(q_zero), ("gx", "gy", "gz"))
    x_waves = wave_squared(jnp.arange(full_x, dtype=jnp.int32), full_x)
    slab_rows = size_x // (groups_y * groups_z)
    thetas = build_thetas(density, q_zero, q_top, qpoints)
    joined = lax.all_to_all(
        thetas.reshape(qpoints, size_x, 1, size_y, size_z),
        ("gy", "gz"),
        split_axis=1,
        concat_axis=2,
        tiled=True,
    )
    planes = join_planes(joined, qpoints, slab_rows, groups_y, groups_z)
    spectra = along_y(forward_z(planes), -1.0)
    plane_part = full_y * full_z // (groups_x * groups_y * groups_z)
    xlines = lax.all_to_all(
        spectra.reshape(2, qpoints, slab_rows, full_y * full_z),
        ("gx", "gy", "gz"),
        split_axis=3,
        concat_axis=2,
        tiled=True,
    )
    flat_index = lax.axis_index(("gx", "gy", "gz")) * plane_part + jnp.arange(
        plane_part, dtype=jnp.int32
    )
    k_squared = (
        x_waves[:, None]
        + (wave_squared(flat_index // full_z, full_y) + wave_squared(flat_index % full_z, full_z))[
            None, :
        ]
    )
    products = along_x(apply_kernel(along_x(xlines, -1.0), k_squared, coupling, q_top), 1.0)
    returned = lax.all_to_all(
        products, ("gx", "gy", "gz"), split_axis=2, concat_axis=3, tiled=True
    ).reshape(2, qpoints, slab_rows, full_y, full_z)
    fields = inverse_z(along_y(returned, 1.0)) * scale_inv
    spread = fields.reshape(qpoints, slab_rows, groups_y, size_y, groups_z, size_z)
    spread = spread.transpose(0, 1, 2, 4, 3, 5).reshape(
        qpoints, slab_rows, groups_y * groups_z, size_y, size_z
    )
    blocks = lax.all_to_all(spread, ("gy", "gz"), split_axis=2, concat_axis=1, tiled=True)
    return blocks.reshape(qpoints, size_x, size_y, size_z)


def solution(mesh):
    placed = (P("gx", "gy", "gz"), P())
    return jax.shard_map(
        body, mesh=mesh, in_specs=placed, out_specs=P(None, "gx", "gy", "gz"), check_vma=False
    )
```

profile of v0, /device:TPU:0, one launch (start us, length us, event | category | flops | bytes accessed | tf_op | source)
XLA Modules:
  0.0 683.0 jit_solution(6947540007924352375)
XLA Ops:
  0.8 3.0 collective-permute-start.1
  7.5 3.7 collective-permute-start.2
  12.7 4.1 collective-permute-done.3
  17.5 4.8 collective-permute-done.4
  22.3 3.0 collective-permute-done.5
  26.5 37.1 %pmax.7 = f32[]{:T(128)} all-reduce(f32[]{:T(128)} %get-tuple-element.178), channel_id=1, replica_groups=mesh['gx'=2,'gy'=4,'gz'=4] {'gx','gy','gz'}, use_global_device_ids=true, to_apply=%region_1.0 | all-reduce | flops 1 | bytes 8 | tf_op jit(solution)/shard_map/pmax | solution.py:155
  64.2 2.7 convolution_multiply_fusion
  68.8 6.3 all-to-all-start
  75.4 5.3 sine_negate_fusion.1
  80.7 30.8 %all-to-all-done = f32[14,16,1,16,128]{4,3,0,2,1:T(8,128)S(1)} async-done(((f32[14,16,1,16,128]{4,3,0,2,1:T(8,128)}), f32[14,16,1,16,128]{4,3,0,2,1:T(8,128)S(1)}, u32[]{:S(2)}, u32[]{:S(2)}) %all-to-all-start) | async-done | bytes 1835040 | tf_op jit(solution)/shard_map/all_to_all | solution.py:159
  111.5 2.4 copy.57
  113.9 2.2 reshape.462
  116.1 7.6 %fusion.28 = f32[2,14,64,512,1]{3,2,1,0,4:T(8,128)S(1)} fusion(f32[14,64,512,1]{2,1,0,3:T(8,128)S(1)} %reshape.462, f32[512,1,512]{2,0,1:T(8,128)S(1)} %get-tuple-element.209, f32[512,1,512]{2,0,1:T(8,128)} %get-tuple-element.210), kind=kOutput, calls=%fused_computation.36 | convolution fusion | flops 5637668864 | bytes 7602176 | tf_op jit(solution)/shard_map/aryz,zpk->paryk/dot_general | solution.py:106
  123.7 5.8 fusion.29
  129.5 26.4 %copy.41 = f32[2,14,1,64,512]{1,0,4,3,2:T(2,128)} copy(f32[2,14,1,64,512]{4,3,0,1,2:T(8,128)} %fusion.29) | data formatting | bytes 7340032 | tf_op jit(solution)/shard_map/reshape | solution.py:170
  155.9 56.7 %reshape.479 = f32[32,1,28672]{2,1,0:T(1,128)} reshape(f32[32768,1,2,14]{3,2,1,0:T(2,128)} %bitcast.123) | data formatting | bytes 7340032
  212.6 9.8 %all-to-all-start.1 = ((f32[32,1,28672]{2,1,0:T(1,128)}), f32[32,1,28672]{2,1,0:T(1,128)}, u32[]{:S(2)}, u32[]{:S(2)}) async-start(f32[32,1,28672]{2,1,0:T(1,128)} %reshape.479), calls=%async_computation.1 | async-start | bytes 7340032 | tf_op jit(solution)/shard_map/all_to_all | solution.py:169
  223.4 82.7 %all-to-all-done.1 = f32[32,1,28672]{2,1,0:T(1,128)} async-done(((f32[32,1,28672]{2,1,0:T(1,128)}), f32[32,1,28672]{2,1,0:T(1,128)}, u32[]{:S(2)}, u32[]{:S(2)}) %all-to-all-start.1) | async-done | bytes 3670048 | tf_op jit(solution)/shard_map/all_to_all | solution.py:169
  306.7 12.8 %reduce = f32[32,28672]{1,0:T(8,128)} reduce(f32[32,1,28672]{2,1,0:T(1,128)} %all-to-all-done.1, f32[]{:T(128)} %broadcast.803), dimensions={1}, to_apply=%all_to_all.11.reduce_sub_computation | reduce | bytes 7340036 | tf_op jit(solution)/shard_map/all_to_all | solution.py:169
  319.5 72.2 %reshape.480 = f32[32768,1,2,14]{3,2,1,0:T(2,128)} reshape(f32[32,28672]{1,0:T(8,128)} %reduce) | data formatting | bytes 7340032
  391.7 28.0 %copy.32 = f32[2,14,32,1024,1]{3,2,0,4,1:T(8,128)} copy(f32[2,14,32,1024,1]{1,0,3,2,4:T(2,128)} %bitcast.124) | data formatting | bytes 7340032 | tf_op jit(solution)/shard_map/all_to_all | solution.py:169
  419.7 6.4 convolution_bitcast_fusion
  426.1 85.2 %while.14 = (s32[]{:T(128)}, f32[2,14,32,1024]{3,2,1,0:T(8,128)}, f32[14,14]{0,1:T(8,128)S(1)}, f32[14,14]{0,1:T(8,128)S(1)}, f32[2,14,32,1024]{3,2,0,1:T(8,128)...) while((s32[]{:T(128)}, f32[2,14,32,1024]{3,2,1,0:T(8,128)}, ...), condition=%wide.region_3.4_spmd.clone, body=%wide.region_2.3_spmd.clone.sunk | while | flops 4620291 | bytes 12063295 | solution.py:138
  428.0 2.7 select_add_fusion.2
  432.2 4.8 select_add_fusion.2
  438.4 4.8 select_add_fusion.2
  444.6 4.8 select_add_fusion.2
  450.8 4.8 select_add_fusion.2
  457.0 4.8 select_add_fusion.2
  463.2 4.8 select_add_fusion.2
  469.4 4.8 select_add_fusion.2
  475.6 4.8 select_add_fusion.2
  481.8 4.8 select_add_fusion.2
  488.0 4.8 select_add_fusion.2
  494.2 4.8 select_add_fusion.2
  500.4 4.8 select_add_fusion.2
  506.6 4.8 select_add_fusion.2
  511.3 6.6 fusion.32
  517.9 4.7 copy.25
  522.6 3.7 all-to-all-start.2
  526.4 4.1 sine_negate_fusion
  530.5 79.5 %all-to-all-done.2 = f32[2,14,32,1024]{3,0,1,2:T(2,128)} async-done(((f32[2,14,32,1024]{3,0,1,2:T(2,128)}), f32[2,14,32,1024]{3,0,1,2:T(2,128)}, u32[]{:S(2)}, u32[]{:S(2)}) %all-to-all-start.2) | async-done | bytes 3670048 | tf_op jit(solution)/shard_map/all_to_all | solution.py:186
  610.0 6.0 copy.26
  616.0 4.9 reshape.472
  621.0 6.0 fusion.6
  627.0 7.1 %bitcast_multiply_fusion = f32[14,64,512]{2,1,0:T(8,128)} fusion(f32[1,512,512]{2,1,0:T(8,128)S(1)} %get-tuple-element.215, f32[1,512,512]{2,1,0:T(8,128)S(1)} %get-tuple-element.216, f32[14,512,2,64,1]{1,3,4,2,0:T(8,128)S(1)} %fusion.6), kind=kOutput, calls=%fused_computation.40 | convolution fusion | flops 5638127616 | bytes 7602176 | tf_op jit(solution)/shard_map/paryz,pzk->aryk/dot_general | solution.py:122
  634.1 1.9 reshape.456
  636.1 45.2 %all_to_all.19 = f32[14,1,16,16,128]{4,3,0,1,2:T(8,128)S(1)} all-to-all(f32[14,1,16,16,128]{4,3,0,1,2:T(8,128)S(1)} %bitcast.130), channel_id=1, replica_groups=mesh['gx'=2,'gy'=4,'gz'=4] {'gy','gz'}, dimensions={2} | all-to-all | bytes 3670016 | tf_op jit(solution)/shard_map/all_to_all | solution.py:194
  (95 shorter events, 33.9 us)
Async XLA Ops:
  0.0 25.3 %copy-start = (f32[16,16,128]{2,1,0:T(8,128)S(1)}, f32[16,16,128]{2,1,0:T(8,128)}, u32[]{:S(2)}) copy-start(f32[16,16,128]{2,1,0:T(8,128)} %param.4) | copy-start | bytes 393220
  0.8 4.7 collective-permute-start.1
  3.8 3.7 collective-permute-start
  7.5 5.1 collective-permute-start.2
  11.2 5.6 collective-permute-start.3
  16.9 5.4 collective-permute-start.4
  17.0 8.3 %collective-permute-start.5 = (f32[20,20,2]{2,1,0:T(8,128)S(1)}, f32[20,20,2]{2,1,0:T(8,128)S(1)}, u32[]{:S(2)}, u32[]{:S(2)}) collective-permute-start(f32[20,20,2]{2,1,0:T(8,128)S(1)} %get-tuple-element.183), channel_id=1, source_target_pairs={{0,1},{1,2},{2,3},{3,0},{4,5},{5,6},{6,7},{7,4},{8,9},{9,10},{10,1... | collective-permute-start | bytes 9608 | tf_op jit(solution)/shard_map/ppermute | solution.py:24
  68.8 42.7 %all-to-all-start = ((f32[14,16,1,16,128]{4,3,0,2,1:T(8,128)}), f32[14,16,1,16,128]{4,3,0,2,1:T(8,128)S(1)}, u32[]{:S(2)}, u32[]{:S(2)}) async-start(f32[14,16,1,16,128]{4,3,0,2,1:T(8,128)} %copy.18), calls=%async_computation | async-start | bytes 3670016 | tf_op jit(solution)/shard_map/all_to_all | solution.py:159
  212.6 9.9 %copy-start.1 = (f32[14,14]{1,0:T(8,128)S(1)}, f32[14,14]{1,0:T(8,128)}, u32[]{:S(2)}) copy-start(f32[14,14]{1,0:T(8,128)} %param.5) | copy-start | bytes 2356
  212.6 93.5 %all-to-all-start.1 = ((f32[32,1,28672]{2,1,0:T(1,128)}), f32[32,1,28672]{2,1,0:T(1,128)}, u32[]{:S(2)}, u32[]{:S(2)}) async-start(f32[32,1,28672]{2,1,0:T(1,128)} %reshape.479), calls=%async_computation.1 | async-start | bytes 7340032 | tf_op jit(solution)/shard_map/all_to_all | solution.py:169
  522.6 87.4 %all-to-all-start.2 = ((f32[2,14,32,1024]{3,0,1,2:T(2,128)}), f32[2,14,32,1024]{3,0,1,2:T(2,128)}, u32[]{:S(2)}, u32[]{:S(2)}) async-start(f32[2,14,32,1024]{3,0,1,2:T(2,128)} %copy.25), calls=%async_computation.2 | async-start | bytes 7340032 | tf_op jit(solution)/shard_map/all_to_all | solution.py:186
where the time goes:
time: 693 us; the launch traced here: 683 us
  local copies, waits for them, and re-layouts  225 us (32%)
  waiting for transfers between devices  209 us (30%)
  other arithmetic  96 us (14%)
  blocking collectives  82.2 us (12%)
  matrix products  42.2 us (6%)
  starting transfers between devices  27 us (4%)
    unnamed x11, local copies, waits for them, and re-layouts  130 us
    all_to_all x1, waiting for transfers between devices, body(): lax.all_to_all(spectra.reshape(2, qpoints, slab_rows, full_y * full_z), (...  82.7 us
    all_to_all x1, waiting for transfers between devices, body(): lax.all_to_all(products, ('gx', 'gy', 'gz'), split_axis=2, concat_axis=3,...  79.5 us
    add x14, other arithmetic, add_source(): return summed + factor[None] * spectrum[:, None]  64.5 us
    all_to_all x1, blocking collectives, body(): lax.all_to_all(spread, ('gy', 'gz'), split_axis=2, concat_axis=1, tiled=T...  45.2 us
    pmax x1, blocking collectives, body(): q_top = lax.pmax(jnp.max(q_zero), ('gx', 'gy', 'gz'))  37.1 us
    all_to_all x1, waiting for transfers between devices, body(): lax.all_to_all(thetas.reshape(qpoints, size_x, 1, size_y, size_z), ('gy',...  30.8 us
    all_to_all x2, local copies, waits for them, and re-layouts, body(): lax.all_to_all(spectra.reshape(2, qpoints, slab_rows, full_y * full_z), (...  28.6 us
  transfers between devices with their start and end apart: 9, of which 9 were waited for; matrix products, arithmetic and copies ran while one was open for 2% of the time, Pallas kernels for 0%

commit v1 on v0

v1 whole, which is shorter than its diff:
```python
import math

import jax
import jax.numpy as jnp
import ml_dtypes
import numpy as np
from jax import lax
from jax.experimental import pallas as pl
from jax.experimental.pallas import tpu as pltpu
from jax.sharding import PartitionSpec as P

zab_ratio = 0.8491 / 9.0
q_cut = 5.0
mesh_step = 0.07
range_factor = 1.0
local_weight = 0.25
spline_root = math.sqrt(3.0) - 2.0
vmem_bytes = 60 * 1024 * 1024


def hartley(length):
    ids = np.arange(length)
    angles = 2.0 * np.pi / length * (ids[:, None] * ids[None, :] % length)
    return np.cos(angles) + np.sin(angles)


def split_table(table):
    table = np.asarray(table, np.float32)
    high = table.astype(ml_dtypes.bfloat16)
    low = (table - high.astype(np.float32)).astype(ml_dtypes.bfloat16)
    return jnp.asarray(high), jnp.asarray(low)


def split_value(value):
    high = value.astype(jnp.bfloat16)
    low = (value - high.astype(jnp.float32)).astype(jnp.bfloat16)
    return high, low


def mul(left, right):
    def dot(a, b):
        return jnp.dot(a, b, preferred_element_type=jnp.float32)

    return dot(left[0], right[0]) + (dot(left[0], right[1]) + dot(left[1], right[0]))


def wave_squared(length):
    ids = np.arange(length)
    folded = np.where(2 * ids < length, ids, ids - length)
    wavenum = (2.0 * np.pi / length) * folded
    return (wavenum * wavenum).astype(np.float32)


def spline_matrix(qpoints):
    knots = np.arange(-1, qpoints + 1)
    nodes = np.arange(qpoints)
    return math.sqrt(3.0) * spline_root ** np.abs(knots[None, :] - nodes[:, None]).astype(np.float64)


def saturated_wavevector(density, grad_sq):
    fermi_k = jnp.cbrt(3.0 * math.pi * math.pi * density)
    reduced = grad_sq / (4.0 * fermi_k * fermi_k * density * density)
    raw_q = fermi_k * (1.0 + zab_ratio * reduced)
    scaled = raw_q / q_cut
    powered = scaled
    series = jnp.zeros_like(scaled)
    for term_order in range(1, 13):
        series = series + powered / term_order
        powered = powered * scaled
    return q_cut * (1.0 - jnp.exp(-series))


def with_halo(cells, axis, count, dim):
    size = cells.shape[dim]
    head = lax.slice_in_dim(cells, 0, 2, axis=dim)
    tail = lax.slice_in_dim(cells, size - 2, size, axis=dim)
    before = lax.ppermute(tail, axis, [(i, (i + 1) % count) for i in range(count)])
    after = lax.ppermute(head, axis, [((i + 1) % count, i) for i in range(count)])
    return jnp.concatenate([before, cells, after], axis=dim)


def slope_squared(padded, dim):
    size = padded.shape[dim] - 4

    def at(offset):
        return lax.slice_in_dim(padded, 2 + offset, 2 + offset + size, axis=dim)

    slope = (8.0 * (at(1) - at(-1)) - (at(2) - at(-2))) / 12.0
    return slope * slope


def global_max(value, axes):
    for axis in axes:
        count = lax.axis_size(axis)
        shifted = [
            lax.ppermute(value, axis, [(i, (i + step) % count) for i in range(count)])
            for step in range(1, count)
        ]
        for other in shifted:
            value = jnp.maximum(value, other)
    return value


def theta_kernel(qpoints, groups, weights, dens_ref, pos_ref, high_ref, low_ref, out_ref, spline_ref, theta_ref):
    rows, full = dens_ref.shape
    part = full // groups
    position = pos_ref[...]
    for knot in range(qpoints + 2):
        offset = jnp.abs(position - float(knot - 1))
        outer = jnp.maximum(2.0 - offset, 0.0)
        inner = jnp.maximum(1.0 - offset, 0.0)
        spline_ref[knot] = (outer * outer * outer - 4.0 * (inner * inner * inner)) / 6.0
    for row in range(0, rows, 8):
        picked = pl.ds(row, 8)
        density = dens_ref[picked, :]
        for node in range(qpoints):
            total = weights[node][0] * spline_ref[0, picked, :]
            for knot in range(1, qpoints + 2):
                total = total + weights[node][knot] * spline_ref[knot, picked, :]
            theta_ref[pl.ds(node * rows + row, 8), :] = total * density
    table = (high_ref[...], low_ref[...])

    def transform(step, carry):
        chunk = theta_ref[pl.ds(pl.multiple_of(step * 2 * rows, 8), 2 * rows), :]
        product = mul(split_value(chunk), table)
        for group in range(groups):
            piece = product[:, group * part : (group + 1) * part]
            out_ref[group, pl.ds(2 * step, 2)] = piece.reshape(2, rows, part)
        return carry

    lax.fori_loop(0, qpoints // 2, transform, 0)


def line_kernel(high_ref, low_ref, in_ref, out_ref):
    groups_in, fields, rows_in, lanes = in_ref.shape
    groups_out, _, rows_out, _ = out_ref.shape
    table = (high_ref[...], low_ref[...])
    for field in range(fields):
        data = in_ref[:, field].reshape(groups_in * rows_in, lanes)
        product = mul(table, split_value(data))
        out_ref[:, field] = product.reshape(groups_out, rows_out, lanes)


def product_kernel(coup_ref, mass_ref, high_ref, low_ref, wave_ref, in_ref, out_ref, spec_ref):
    groups, qpoints, rows, lanes = in_ref.shape
    total_rows = groups * rows
    table = (high_ref[...], low_ref[...])
    for field in range(qpoints):
        data = in_ref[:, field].reshape(total_rows, lanes)
        spec_ref[field] = mul(table, split_value(data))

    def couple(step, carry):
        picked = pl.ds(pl.multiple_of(step * 8, 8), 8)
        waves = wave_ref[picked, :]
        spectra = [spec_ref[field, picked, :] for field in range(qpoints)]
        sums = [None] * qpoints
        for level in range(2 * qpoints - 1):
            mass = mass_ref[level]
            factor = local_weight + mass / (waves + mass)
            for target in range(max(0, level - qpoints + 1), min(qpoints, level + 1)):
                source = level - target
                term = (coup_ref[target, source] * factor) * spectra[source]
                sums[target] = term if sums[target] is None else sums[target] + term
        for field in range(qpoints):
            spec_ref[field, picked, :] = sums[field]
        return carry

    lax.fori_loop(0, total_rows // 8, couple, 0)
    for field in range(qpoints):
        product = mul(table, split_value(spec_ref[field]))
        out_ref[:, field] = product.reshape(groups, rows, lanes)


def inverse_z_kernel(high_ref, low_ref, in_ref, out_ref):
    groups, fields, rows, part = in_ref.shape
    table = (high_ref[...], low_ref[...])

    def transform(step, carry):
        picked = pl.ds(2 * step, 2)
        pieces = [in_ref[group, picked].reshape(2 * rows, part) for group in range(groups)]
        product = mul(split_value(jnp.concatenate(pieces, axis=1)), table)
        groups_out, _, _, part_out = out_ref.shape
        for group in range(groups_out):
            piece = product[:, group * part_out : (group + 1) * part_out]
            out_ref[group, picked] = piece.reshape(2, rows, part_out)
        return carry

    lax.fori_loop(0, fields // 2, transform, 0)


def call(kernel, shape, specs, scratch=()):
    return pl.pallas_call(
        kernel,
        out_shape=jax.ShapeDtypeStruct(shape, jnp.float32),
        in_specs=[pl.BlockSpec(memory_space=space) for space in specs],
        out_specs=pl.BlockSpec(memory_space=pltpu.VMEM),
        scratch_shapes=list(scratch),
        compiler_params=pltpu.CompilerParams(vmem_limit_bytes=vmem_bytes),
    )


def exchange(value, axes):
    return lax.all_to_all(value, axes, split_axis=0, concat_axis=0, tiled=True)


def body(density, coupling):
    size_x, size_y, size_z = density.shape
    qpoints = coupling.shape[0]
    groups_x, groups_y, groups_z = (lax.axis_size("gx"), lax.axis_size("gy"), lax.axis_size("gz"))
    full_x, full_y, full_z = (size_x * groups_x, size_y * groups_y, size_z * groups_z)
    slab = size_x // groups_z
    groups_xz = groups_x * groups_z
    part_y = full_y // groups_xz
    part_z = full_z // groups_y
    vmem, smem = pltpu.VMEM, pltpu.SMEM

    lines = exchange(density.reshape(groups_z, slab, size_y, size_z), "gz")
    lines = lines.transpose(1, 2, 0, 3).reshape(slab, size_y, full_z)
    grad_sq = (
        slope_squared(with_halo(lines, ("gx", "gz"), groups_xz, 0), 0)
        + slope_squared(with_halo(lines, "gy", groups_y, 1), 1)
        + slope_squared(jnp.concatenate([lines[..., -2:], lines, lines[..., :2]], axis=2), 2)
    )
    q_zero = saturated_wavevector(lines, grad_sq)
    q_top = global_max(jnp.max(q_zero).reshape(1, 1), ("gz", "gy", "gx"))
    position = jnp.maximum(qpoints - 1.0 + jnp.log(q_zero / q_top) / mesh_step, 0.0)

    rows = slab * size_y
    z_table = hartley(full_z)
    weights = [[float(np.float32(w)) for w in line] for line in spline_matrix(qpoints)]

    def thetas(*refs):
        theta_kernel(qpoints, groups_y, weights, *refs)

    spectra = call(
        thetas,
        (groups_y, qpoints, rows, part_z),
        [vmem] * 4,
        [pltpu.VMEM((qpoints + 2, rows, full_z), jnp.float32), pltpu.VMEM((qpoints * rows, full_z), jnp.float32)],
    )(lines.reshape(rows, full_z), position.reshape(rows, full_z), *split_table(z_table))
    spectra = exchange(spectra, "gy")

    y_table = hartley(full_y).reshape(groups_xz, part_y, groups_y, size_y)
    y_matrix = np.einsum("gkhy,st->gskhty", y_table, np.eye(slab))
    y_matrix = y_matrix.reshape(groups_xz * slab * part_y, groups_y * rows)
    short = slab * part_y
    spectra = call(line_kernel, (groups_xz, qpoints, short, part_z), [vmem] * 3)(*split_table(y_matrix), spectra)
    spectra = exchange(spectra, ("gx", "gz"))

    x_matrix = np.kron(hartley(full_x), np.eye(part_y))
    y_first = lax.axis_index(("gx", "gz")) * part_y
    z_first = lax.axis_index("gy") * part_z
    y_waves = lax.dynamic_slice_in_dim(jnp.asarray(wave_squared(full_y)), y_first, part_y)
    z_waves = lax.dynamic_slice_in_dim(jnp.asarray(wave_squared(full_z)), z_first, part_z)
    x_waves = jnp.asarray(wave_squared(full_x))
    waves = (x_waves[:, None, None] + y_waves[None, :, None] + z_waves[None, None, :]).reshape(-1, part_z)
    levels = jnp.asarray(np.exp(-mesh_step * (2 * qpoints - 2 - np.arange(2 * qpoints - 1))), jnp.float32)
    masses = (range_factor * q_top.reshape(()) * q_top.reshape(())) * levels
    products = call(
        product_kernel,
        spectra.shape,
        [smem, smem, vmem, vmem, vmem, vmem],
        [pltpu.VMEM((qpoints, groups_xz * short, part_z), jnp.float32)],
    )(coupling, masses, *split_table(x_matrix), waves, spectra)
    returned = exchange(products, ("gx", "gz"))

    fields = call(line_kernel, (groups_y, qpoints, rows, part_z), [vmem] * 3)(*split_table(y_matrix.T), returned)
    fields = exchange(fields, "gy")
    scaled = z_table / (full_x * full_y * full_z)
    fields = call(inverse_z_kernel, (groups_z, qpoints, rows, size_z), [vmem] * 3)(*split_table(scaled), fields)
    blocks = exchange(fields, "gz")
    blocks = blocks.reshape(groups_z, qpoints, slab, size_y, size_z)
    return blocks.transpose(1, 0, 2, 3, 4).reshape(qpoints, size_x, size_y, size_z)


def solution(mesh):
    placed = (P("gx", "gy", "gz"), P())
    return jax.shard_map(
        body, mesh=mesh, in_specs=placed, out_specs=P(None, "gx", "gy", "gz"), check_vma=False
    )
```

time: 693 us -> 252 us (0.36); the launches traced: 683 us -> 251 us
  local copies, waits for them, and re-layouts: 225 us -> 4.61 us
  waiting for transfers between devices: 209 us -> 27.2 us
  other arithmetic: 96 us -> 3.11 us
  blocking collectives: 82.2 us -> 154 us
  matrix products: 42.2 us -> 0 us
  Pallas kernels: 0 us -> 34 us
    all_to_all x3 -> x1, waiting for transfers between devices: 193 us -> 20.4 us  [exchange(): return lax.all_to_all(value, axes, split_axis=0, concat_axis=0, tiled=True)]
    unnamed x11 -> x12, local copies, waits for them, and re-layouts: 130 us -> 1.95 us
    all_to_all x1 -> x5, blocking collectives: 45.2 us -> 154 us  [exchange(): return lax.all_to_all(value, axes, split_axis=0, concat_axis=0, tiled=True)]
    add x30 -> x2, other arithmetic: 65.6 us -> 0.75 us  [body(): x_waves[:, None, None] + y_waves[None, :, None] + z_waves[None, None, :]]
    dot_general x7 -> x0, matrix products: 42.2 us -> none  [the longest x2 13.1 us: along_x(): jnp.einsum('pkqx,qaxm->pakm', matrix, complex_pair, precision=highest)]
    pmax x1 -> x0, blocking collectives: 37.1 us -> none  [body(): q_top = lax.pmax(jnp.max(q_zero), ('gx', 'gy', 'gz'))]
    all_to_all x3 -> x0, local copies, waits for them, and re-layouts: 34.6 us -> none  [the longest x2 28.6 us: body(): lax.all_to_all(spectra.reshape(2, qpoints, slab_rows, full_y * full_z), (...]
    pallas_call x0 -> x5, Pallas kernels: none -> 34 us  [the longest x1 10.3 us: body(): call(product_kernel, spectra.shape, [smem, smem, vmem, vmem, vmem, vmem],...]
  transfers between devices with their start and end apart: 9 -> 12, of which waited for: 9 -> 5; matrix products, arithmetic and copies ran while one was open for 2% -> 1% of each run, Pallas kernels for 0% -> 0%
where the time goes in v1:
time: 252 us; the launch traced here: 251 us
  blocking collectives  154 us (61%)
  Pallas kernels  34 us (13%)
  waiting for transfers between devices  27.2 us (11%)
  starting transfers between devices  22.7 us (9%)
  between operations  5.48 us (2%)
  local copies, waits for them, and re-layouts  4.61 us (2%)
  other arithmetic  3.11 us (1%)
    all_to_all x5, blocking collectives, exchange(): return lax.all_to_all(value, axes, split_axis=0, concat_axis=0, tiled=True)  154 us
    all_to_all x1, waiting for transfers between devices, exchange(): return lax.all_to_all(value, axes, split_axis=0, concat_axis=0, tiled=True)  20.4 us
    ppermute x7, starting transfers between devices, global_max(): lax.ppermute(value, axis, [(i, (i + step) % count) for i in range(count)])  12.4 us
    pallas_call x1, Pallas kernels, body(): call(product_kernel, spectra.shape, [smem, smem, vmem, vmem, vmem, vmem],...  10.3 us
    pallas_call x1, Pallas kernels, body(): call(thetas, (groups_y, qpoints, rows, part_z), [vmem] * 4, [pltpu.VMEM((...  8.82 us
    ppermute x2, starting transfers between devices, with_halo(): lax.ppermute(head, axis, [((i + 1) % count, i) for i in range(count)])  6.5 us
    pallas_call x1, Pallas kernels, body(): call(inverse_z_kernel, (groups_z, qpoints, rows, size_z), [vmem] * 3)  5.87 us
  transfers between devices with their start and end apart: 12, of which 5 were waited for; matrix products, arithmetic and copies ran while one was open for 1% of the time, Pallas kernels for 0%

profile of v1, /device:TPU:0, one launch (start us, length us, event | category | flops | bytes accessed | tf_op | source)
XLA Modules:
  0.0 250.9 jit_solution(14407871419694140857)
XLA Ops:
  0.0 8.9 %all_to_all.30 = f32[4,4,16,128]{3,2,1,0:T(8,128)S(1)} all-to-all(f32[4,4,16,128]{3,2,1,0:T(8,128)} %bitcast.45), channel_id=1, replica_groups=mesh['gx'=2,'gy'=4,'gz'=4] {'gz'}, dimensions={0} | all-to-all | bytes 262144 | tf_op jit(solution)/shard_map/all_to_all | solution.py:203
  8.9 0.1 collective-permute-start.1
  9.0 0.1 fusion.54
  9.1 0.1 copy.23
  9.2 4.2 %collective-permute-start.2 = (f32[4,2,512]{2,1,0:T(2,128)S(1)}, f32[4,2,512]{2,1,0:T(2,128)S(1)}, u32[]{:S(2)}, u32[]{:S(2)}) collective-permute-start(f32[4,2,512]{2,1,0:T(2,128)S(1)} %get-tuple-element.12), channel_id=1, source_target_pairs={{4,0},{8,4},{12,8},{0,12},{5,1},{9,5},{13,9},{1,13},{6,2},{10,6},{... | collective-permute-start | bytes 49160 | tf_op jit(solution)/shard_map/ppermute | solution.py:78
  13.3 2.3 collective-permute-start
  15.7 0.0 collective-permute-start.3
  15.7 0.7 copy.42
  16.3 0.0 collective-permute-done.1
  16.4 1.2 collective-permute-done
  17.6 0.0 collective-permute-done.2
  17.6 3.6 %collective-permute-done.3 = f32[4,2,512]{2,1,0:T(2,128)S(1)} collective-permute-done((f32[4,2,512]{2,1,0:T(2,128)S(1)}, f32[4,2,512]{2,1,0:T(2,128)S(1)}, u32[]{:S(2)}, u32[]{:S(2)}) %collective-permute-start.3) | collective-permute-done | bytes 16416 | tf_op jit(solution)/shard_map/ppermute | solution.py:77
  21.2 1.1 fusion.51
  22.3 0.0 collective-permute-start.4
  22.3 0.0 collective-permute-start.5
  22.3 1.7 collective-permute-start.6
  24.1 1.3 collective-permute-done.4
  26.7 0.0 collective-permute-done.5
  27.4 0.0 collective-permute-done.6
  28.1 1.4 collective-permute-start.7
  29.4 1.6 collective-permute-start.8
  31.0 4.8 %collective-permute-start.9 = (f32[1,1]{1,0:T(1,128)}, f32[1,1]{1,0:T(1,128)}, u32[]{:S(2)}, u32[]{:S(2)}) collective-permute-start(f32[1,1]{1,0:T(1,128)} %max.29), channel_id=1, source_target_pairs={{0,12},{4,0},{8,4},{12,8},{1,13},{5,1},{9,5},{13,9},{2,14},{6,2},{... | collective-permute-start | bytes 20 | tf_op jit(solution)/shard_map/ppermute | solution.py:96
  37.8 2.9 %collective-permute-start.10 = (f32[1,1]{1,0:T(1,128)}, f32[1,1]{1,0:T(1,128)}, u32[]{:S(2)}, u32[]{:S(2)}) collective-permute-start(f32[1,1]{1,0:T(1,128)} %max.32), channel_id=1, source_target_pairs={{0,16},{16,0},{1,17},{17,1},{2,18},{18,2},{3,19},{19,3},{4,20},{20... | collective-permute-start | bytes 20 | tf_op jit(solution)/shard_map/ppermute | solution.py:96
  40.7 0.7 collective-permute-done.10
  42.1 0.7 add_maximum_fusion
  42.8 8.8 %shard_map.154 = f32[4,14,64,128]{3,2,1,0:T(8,128)} custom-call(f32[64,512]{1,0:T(8,128)} %bitcast.42, f32[64,512]{1,0:T(8,128)} %bitcast.43, bf16[512,512]{1,0:T(8,128)(2,1)} %constant.108.clone.refs_2_, bf16[512,512]{1,0:T(8,128)(2,1)} %constant.109.clone.refs_3_), custom_call_target="tpu_custom_call" | custom-call | tf_op jit(solution)/shard_map/pallas_call | solution.py:235
  51.6 44.0 %all_to_all.31.in_ref = f32[4,14,64,128]{3,2,1,0:T(8,128)} all-to-all(f32[4,14,64,128]{3,2,1,0:T(8,128)} %shard_map.154), channel_id=1, replica_groups=mesh['gx'=2,'gy'=4,'gz'=4] {'gy'}, dimensions={0} | all-to-all | bytes 3670016 | tf_op jit(solution)/shard_map/all_to_all | solution.py:203
  95.6 4.5 %shard_map.155 = f32[8,14,32,128]{3,2,1,0:T(8,128)} custom-call(bf16[256,256]{1,0:T(8,128)(2,1)} %constant.110.clone.high_ref, bf16[256,256]{1,0:T(8,128)(2,1)} %constant.111.clone.low_ref, f32[4,14,64,128]{3,2,1,0:T(8,128)} %all_to_all.31.in_ref), custom_call_target="tpu_custom_call" | custom-call | tf_op jit(solution)/shard_map/pallas_call | solution.py:247
  100.1 3.7 %all-to-all-start.2 = ((f32[8,14,32,128]{3,2,1,0:T(8,128)}), f32[8,14,32,128]{3,2,1,0:T(8,128)S(1)}, u32[]{:S(2)}, u32[]{:S(2)}) async-start(f32[8,14,32,128]{3,2,1,0:T(8,128)} %shard_map.155), calls=%async_computation.2 | async-start | bytes 3670016 | tf_op jit(solution)/shard_map/all_to_all | solution.py:203
  103.8 0.0 copy-done.3
  103.8 0.1 dynamic_slice.6
  103.9 0.1 add.112
  104.0 0.0 copy-done.1
  104.0 0.1 add.107
  104.1 0.1 add.108
  104.2 0.8 dynamic_slice.7
  105.0 0.7 broadcast_add_fusion.wave_ref
  105.7 0.0 copy-done.2
  105.7 0.6 broadcast_multiply_fusion.mass_ref
  106.3 20.4 %all-to-all-done.2.in_ref = f32[8,14,32,128]{3,2,1,0:T(8,128)S(1)} async-done(((f32[8,14,32,128]{3,2,1,0:T(8,128)}), f32[8,14,32,128]{3,2,1,0:T(8,128)S(1)}, u32[]{:S(2)}, u32[]{:S(2)}) %all-to-all-start.2) | async-done | bytes 1835040 | tf_op jit(solution)/shard_map/all_to_all | solution.py:203
  126.7 1.2 copy-done
  127.9 10.3 %shard_map.156 = f32[8,14,32,128]{3,2,1,0:T(8,128)} custom-call(f32[14,14]{1,0:T(8,128)} %coup_ref.1, f32[27]{0:T(128)} %broadcast_multiply_fusion.mass_ref, bf16[256,256]{1,0:T(8,128)(2,1)} %constant.116.clone.high_ref, bf16[256,256]{1,0:T(8,128)(2,1)} %constant.117.clone.low_ref, f32[256,128]{1,0:T(8,128)} %broadcast_add_fusion.wave_ref, ...), custom_call_target="tpu_custom_call" | custom-call | tf_op jit(solution)/shard_map/pallas_call | solution.py:259
  138.2 27.5 %all_to_all.32.in_ref = f32[8,14,32,128]{3,2,1,0:T(8,128)} all-to-all(f32[8,14,32,128]{3,2,1,0:T(8,128)} %shard_map.156), channel_id=1, replica_groups=mesh['gx'=2,'gy'=4,'gz'=4] {'gx','gz'}, dimensions={0} | all-to-all | bytes 3670016 | tf_op jit(solution)/shard_map/all_to_all | solution.py:203
  165.7 4.5 %shard_map.157 = f32[4,14,64,128]{3,2,1,0:T(8,128)} custom-call(bf16[256,256]{1,0:T(8,128)(2,1)} %constant.118.clone.high_ref, bf16[256,256]{1,0:T(8,128)(2,1)} %constant.119.clone.low_ref, f32[8,14,32,128]{3,2,1,0:T(8,128)} %all_to_all.32.in_ref), custom_call_target="tpu_custom_call" | custom-call | tf_op jit(solution)/shard_map/pallas_call | solution.py:267
  170.2 47.1 %all_to_all.33.in_ref = f32[4,14,64,128]{3,2,1,0:T(8,128)} all-to-all(f32[4,14,64,128]{3,2,1,0:T(8,128)} %shard_map.157), channel_id=1, replica_groups=mesh['gx'=2,'gy'=4,'gz'=4] {'gy'}, dimensions={0} | all-to-all | bytes 3670016 | tf_op jit(solution)/shard_map/all_to_all | solution.py:203
  217.3 5.9 %shard_map.158 = f32[4,14,64,128]{3,2,1,0:T(8,128)} custom-call(bf16[512,512]{1,0:T(8,128)(2,1)} %constant.120.clone.high_ref, bf16[512,512]{1,0:T(8,128)(2,1)} %constant.121.clone.low_ref, f32[4,14,64,128]{3,2,1,0:T(8,128)} %all_to_all.33.in_ref), custom_call_target="tpu_custom_call" | custom-call | tf_op jit(solution)/shard_map/pallas_call | solution.py:270
  223.2 26.4 %all_to_all.34 = f32[4,14,64,128]{3,2,1,0:T(8,128)S(1)} all-to-all(f32[4,14,64,128]{3,2,1,0:T(8,128)} %shard_map.158), channel_id=1, replica_groups=mesh['gx'=2,'gy'=4,'gz'=4] {'gz'}, dimensions={0} | all-to-all | bytes 3670016 | tf_op jit(solution)/shard_map/all_to_all | solution.py:203
  249.6 1.3 copy.27
  (18 shorter events, 0.1 us)
Async XLA Ops:
  8.9 7.5 %collective-permute-start.1 = (f32[2,16,512]{2,1,0:T(8,128)S(1)}, f32[2,16,512]{2,1,0:T(8,128)S(1)}, u32[]{:S(2)}, u32[]{:S(2)}) collective-permute-start(f32[2,16,512]{2,1,0:T(8,128)S(1)} %bitcast.46), channel_id=1, source_target_pairs={{0,1},{1,2},{2,3},{3,16},{16,17},{17,18},{18,19},{19,0},{4,5},{5,6... | collective-permute-start | bytes 196616 | tf_op jit(solution)/shard_map/ppermute | solution.py:77
  9.2 8.4 %collective-permute-start.2 = (f32[4,2,512]{2,1,0:T(2,128)S(1)}, f32[4,2,512]{2,1,0:T(2,128)S(1)}, u32[]{:S(2)}, u32[]{:S(2)}) collective-permute-start(f32[4,2,512]{2,1,0:T(2,128)S(1)} %get-tuple-element.12), channel_id=1, source_target_pairs={{4,0},{8,4},{12,8},{0,12},{5,1},{9,5},{13,9},{1,13},{6,2},{10,6},{... | collective-permute-start | bytes 49160 | tf_op jit(solution)/shard_map/ppermute | solution.py:78
  13.3 4.3 %collective-permute-start = (f32[2,16,512]{2,1,0:T(8,128)S(1)}, f32[2,16,512]{2,1,0:T(8,128)S(1)}, u32[]{:S(2)}, u32[]{:S(2)}) collective-permute-start(f32[2,16,512]{2,1,0:T(8,128)S(1)} %bitcast.47), channel_id=1, source_target_pairs={{1,0},{2,1},{3,2},{16,3},{17,16},{18,17},{19,18},{0,19},{5,4},{6,5... | collective-permute-start | bytes 196616 | tf_op jit(solution)/shard_map/ppermute | solution.py:78
  15.7 5.5 %collective-permute-start.3 = (f32[4,2,512]{2,1,0:T(2,128)S(1)}, f32[4,2,512]{2,1,0:T(2,128)S(1)}, u32[]{:S(2)}, u32[]{:S(2)}) collective-permute-start(f32[4,2,512]{2,1,0:T(2,128)S(1)} %get-tuple-element.13), channel_id=1, source_target_pairs={{0,4},{4,8},{8,12},{12,0},{1,5},{5,9},{9,13},{13,1},{2,6},{6,10},{... | collective-permute-start | bytes 49160 | tf_op jit(solution)/shard_map/ppermute | solution.py:77
  22.3 3.1 %collective-permute-start.4 = (f32[1,1]{1,0:T(1,128)}, f32[1,1]{1,0:T(1,128)}, u32[]{:S(2)}, u32[]{:S(2)}) collective-permute-start(f32[1,1]{1,0:T(1,128)} %bitcast.2), channel_id=1, source_target_pairs={{0,1},{1,2},{2,3},{3,0},{4,5},{5,6},{6,7},{7,4},{8,9},{9,10},{10,1... | collective-permute-start | bytes 20 | tf_op jit(solution)/shard_map/ppermute | solution.py:96
  22.3 4.4 %collective-permute-start.5 = (f32[1,1]{1,0:T(1,128)}, f32[1,1]{1,0:T(1,128)}, u32[]{:S(2)}, u32[]{:S(2)}) collective-permute-start(f32[1,1]{1,0:T(1,128)} %bitcast.2), channel_id=1, source_target_pairs={{0,2},{1,3},{2,0},{3,1},{4,6},{5,7},{6,4},{7,5},{8,10},{9,11},{10,... | collective-permute-start | bytes 20 | tf_op jit(solution)/shard_map/ppermute | solution.py:96
  22.3 5.1 %collective-permute-start.6 = (f32[1,1]{1,0:T(1,128)}, f32[1,1]{1,0:T(1,128)}, u32[]{:S(2)}, u32[]{:S(2)}) collective-permute-start(f32[1,1]{1,0:T(1,128)} %bitcast.2), channel_id=1, source_target_pairs={{0,3},{1,0},{2,1},{3,2},{4,7},{5,4},{6,5},{7,6},{8,11},{9,8},{10,9... | collective-permute-start | bytes 20 | tf_op jit(solution)/shard_map/ppermute | solution.py:96
  28.1 7.8 %collective-permute-start.7 = (f32[1,1]{1,0:T(1,128)}, f32[1,1]{1,0:T(1,128)}, u32[]{:S(2)}, u32[]{:S(2)}) collective-permute-start(f32[1,1]{1,0:T(1,128)} %max.29), channel_id=1, source_target_pairs={{0,4},{4,8},{8,12},{12,0},{1,5},{5,9},{9,13},{13,1},{2,6},{6,10},{... | collective-permute-start | bytes 20 | tf_op jit(solution)/shard_map/ppermute | solution.py:96
  29.4 7.1 %collective-permute-start.8 = (f32[1,1]{1,0:T(1,128)}, f32[1,1]{1,0:T(1,128)}, u32[]{:S(2)}, u32[]{:S(2)}) collective-permute-start(f32[1,1]{1,0:T(1,128)} %max.29), channel_id=1, source_target_pairs={{0,8},{4,12},{8,0},{12,4},{1,9},{5,13},{9,1},{13,5},{2,10},{6,14},... | collective-permute-start | bytes 20 | tf_op jit(solution)/shard_map/ppermute | solution.py:96
  31.0 6.2 %collective-permute-start.9 = (f32[1,1]{1,0:T(1,128)}, f32[1,1]{1,0:T(1,128)}, u32[]{:S(2)}, u32[]{:S(2)}) collective-permute-start(f32[1,1]{1,0:T(1,128)} %max.29), channel_id=1, source_target_pairs={{0,12},{4,0},{8,4},{12,8},{1,13},{5,1},{9,5},{13,9},{2,14},{6,2},{... | collective-permute-start | bytes 20 | tf_op jit(solution)/shard_map/ppermute | solution.py:96
  37.8 3.6 %collective-permute-start.10 = (f32[1,1]{1,0:T(1,128)}, f32[1,1]{1,0:T(1,128)}, u32[]{:S(2)}, u32[]{:S(2)}) collective-permute-start(f32[1,1]{1,0:T(1,128)} %max.32), channel_id=1, source_target_pairs={{0,16},{16,0},{1,17},{17,1},{2,18},{18,2},{3,19},{19,3},{4,20},{20... | collective-permute-start | bytes 20 | tf_op jit(solution)/shard_map/ppermute | solution.py:96
  100.1 3.7 %copy-start.3 = (f32[64]{0:T(128)S(1)}, f32[64]{0:T(128)}, u32[]{:S(2)}) copy-start(f32[64]{0:T(128)} %constant.112.clone) | copy-start | bytes 772
  100.1 3.9 %copy-start.1 = (f32[32]{0:T(128)S(1)}, f32[32]{0:T(128)}, u32[]{:S(2)}) copy-start(f32[32]{0:T(128)} %constant.114.clone) | copy-start | bytes 388
  100.1 5.6 %copy-start.2 = (f32[27]{0:T(128)S(1)}, f32[27]{0:T(128)}, u32[]{:S(2)}) copy-start(f32[27]{0:T(128)} %constant.115.clone) | copy-start | bytes 328
  100.1 26.6 %all-to-all-start.2 = ((f32[8,14,32,128]{3,2,1,0:T(8,128)}), f32[8,14,32,128]{3,2,1,0:T(8,128)S(1)}, u32[]{:S(2)}, u32[]{:S(2)}) async-start(f32[8,14,32,128]{3,2,1,0:T(8,128)} %shard_map.155), calls=%async_computation.2 | async-start | bytes 3670016 | tf_op jit(solution)/shard_map/all_to_all | solution.py:203
  126.7 1.2 copy-start

commit v2 on v1

--- a/solution.py
+++ b/solution.py
@@ -101,31 +101,33 @@
     return value
 
 
-def theta_kernel(qpoints, groups, weights, dens_ref, pos_ref, high_ref, low_ref, out_ref, spline_ref, theta_ref):
-    rows, full = dens_ref.shape
-    part = full // groups
+def theta_kernel(qpoints, weights, dens_ref, pos_ref, high_ref, low_ref, out_ref, spline_ref, theta_ref):
+    rows = dens_ref.shape[0]
     position = pos_ref[...]
     for knot in range(qpoints + 2):
         offset = jnp.abs(position - float(knot - 1))
         outer = jnp.maximum(2.0 - offset, 0.0)
         inner = jnp.maximum(1.0 - offset, 0.0)
         spline_ref[knot] = (outer * outer * outer - 4.0 * (inner * inner * inner)) / 6.0
-    for row in range(0, rows, 8):
-        picked = pl.ds(row, 8)
+
+    def build(step, carry):
+        first = pl.multiple_of(step * 8, 8)
+        picked = pl.ds(first, 8)
         density = dens_ref[picked, :]
         for node in range(qpoints):
             total = weights[node][0] * spline_ref[0, picked, :]
             for knot in range(1, qpoints + 2):
                 total = total + weights[node][knot] * spline_ref[knot, picked, :]
-            theta_ref[pl.ds(node * rows + row, 8), :] = total * density
+            theta_ref[pl.ds(node * rows + first, 8), :] = total * density
+        return carry
+
+    lax.fori_loop(0, rows // 8, build, 0)
     table = (high_ref[...], low_ref[...])
 
     def transform(step, carry):
         chunk = theta_ref[pl.ds(pl.multiple_of(step * 2 * rows, 8), 2 * rows), :]
         product = mul(split_value(chunk), table)
-        for group in range(groups):
-            piece = product[:, group * part : (group + 1) * part]
-            out_ref[group, pl.ds(2 * step, 2)] = piece.reshape(2, rows, part)
+        out_ref[0, pl.ds(2 * step, 2)] = product.reshape(2, rows, product.shape[1])
         return carry
 
     lax.fori_loop(0, qpoints // 2, transform, 0)
@@ -216,40 +218,44 @@
 
     lines = exchange(density.reshape(groups_z, slab, size_y, size_z), "gz")
     lines = lines.transpose(1, 2, 0, 3).reshape(slab, size_y, full_z)
+    lines = lax.all_gather(lines, "gy", axis=1, tiled=True)
     grad_sq = (
         slope_squared(with_halo(lines, ("gx", "gz"), groups_xz, 0), 0)
-        + slope_squared(with_halo(lines, "gy", groups_y, 1), 1)
+        + slope_squared(jnp.concatenate([lines[:, -2:], lines, lines[:, :2]], axis=1), 1)
         + slope_squared(jnp.concatenate([lines[..., -2:], lines, lines[..., :2]], axis=2), 2)
     )
     q_zero = saturated_wavevector(lines, grad_sq)
-    q_top = global_max(jnp.max(q_zero).reshape(1, 1), ("gz", "gy", "gx"))
+    q_top = global_max(jnp.max(q_zero).reshape(1, 1), ("gz", "gx"))
     position = jnp.maximum(qpoints - 1.0 + jnp.log(q_zero / q_top) / mesh_step, 0.0)
 
     rows = slab * size_y
+    plane = slab * full_y
+    z_first = lax.axis_index("gy") * part_z
     z_table = hartley(full_z)
     weights = [[float(np.float32(w)) for w in line] for line in spline_matrix(qpoints)]
 
     def thetas(*refs):
-        theta_kernel(qpoints, groups_y, weights, *refs)
-
+        theta_kernel(qpoints, weights, *refs)
+
+    z_parts = [lax.dynamic_slice_in_dim(t, z_first, part_z, axis=1) for t in split_table(z_table)]
     spectra = call(
         thetas,
-        (groups_y, qpoints, rows, part_z),
+        (1, qpoints, plane, part_z),
         [vmem] * 4,
-        [pltpu.VMEM((qpoints + 2, rows, full_z), jnp.float32), pltpu.VMEM((qpoints * rows, full_z), jnp.float32)],
-    )(lines.reshape(rows, full_z), position.reshape(rows, full_z), *split_table(z_table))
-    spectra = exchange(spectra, "gy")
+        [pltpu.VMEM((qpoints + 2, plane, full_z), jnp.float32), pltpu.VMEM((qpoints * plane, full_z), jnp.float32)],
+    )(lines.reshape(plane, full_z), position.reshape(plane, full_z), *z_parts)
 
     y_table = hartley(full_y).reshape(groups_xz, part_y, groups_y, size_y)
     y_matrix = np.einsum("gkhy,st->gskhty", y_table, np.eye(slab))
     y_matrix = y_matrix.reshape(groups_xz * slab * part_y, groups_y * rows)
     short = slab * part_y
-    spectra = call(line_kernel, (groups_xz, qpoints, short, part_z), [vmem] * 3)(*split_table(y_matrix), spectra)
+    y_planes = np.einsum("gky,st->gskty", hartley(full_y).reshape(groups_xz, part_y, full_y), np.eye(slab))
+    y_planes = y_planes.reshape(groups_xz * short, plane)
+    spectra = call(line_kernel, (groups_xz, qpoints, short, part_z), [vmem] * 3)(*split_table(y_planes), spectra)
     spectra = exchange(spectra, ("gx", "gz"))
 
     x_matrix = np.kron(hartley(full_x), np.eye(part_y))
     y_first = lax.axis_index(("gx", "gz")) * part_y
-    z_first = lax.axis_index("gy") * part_z
     y_waves = lax.dynamic_slice_in_dim(jnp.asarray(wave_squared(full_y)), y_first, part_y)
     z_waves = lax.dynamic_slice_in_dim(jnp.asarray(wave_squared(full_z)), z_first, part_z)
     x_waves = jnp.asarray(wave_squared(full_x))
@@ -261,13 +267,12 @@
         spectra.shape,
         [smem, smem, vmem, vmem, vmem, vmem],
         [pltpu.VMEM((qpoints, groups_xz * short, part_z), jnp.float32)],
-    )(coupling, masses, *split_table(x_matrix), waves, spectra)
+    )(coupling / (full_x * full_y * full_z), masses, *split_table(x_matrix), waves, spectra)
     returned = exchange(products, ("gx", "gz"))
 
     fields = call(line_kernel, (groups_y, qpoints, rows, part_z), [vmem] * 3)(*split_table(y_matrix.T), returned)
     fields = exchange(fields, "gy")
-    scaled = z_table / (full_x * full_y * full_z)
-    fields = call(inverse_z_kernel, (groups_z, qpoints, rows, size_z), [vmem] * 3)(*split_table(scaled), fields)
+    fields = call(inverse_z_kernel, (groups_z, qpoints, rows, size_z), [vmem] * 3)(*split_table(z_table), fields)
     blocks = exchange(fields, "gz")
     blocks = blocks.reshape(groups_z, qpoints, slab, size_y, size_z)
     return blocks.transpose(1, 0, 2, 3, 4).reshape(qpoints, size_x, size_y, size_z)

time: 252 us -> 223 us (0.88)
  blocking collectives: 154 us -> 118 us
  Pallas kernels: 34 us -> 43.5 us
  starting transfers between devices: 22.7 us -> 17.5 us
    all_to_all x5 -> x3, blocking collectives: 154 us -> 102 us  [exchange(): return lax.all_to_all(value, axes, split_axis=0, concat_axis=0, tiled=True)]
    all_gather x0 -> x1, blocking collectives: none -> 16.2 us  [body(): lines = lax.all_gather(lines, 'gy', axis=1, tiled=True)]
    pallas_call x1, Pallas kernels: 8.82 us -> 18.3 us  [body(): call(thetas, (1, qpoints, plane, part_z), [vmem] * 4, [pltpu.VMEM((qpoint...]
    ppermute x7 -> x4, starting transfers between devices: 12.4 us -> 6.57 us  [global_max(): lax.ppermute(value, axis, [(i, (i + step) % count) for i in range(count)])]
    all_to_all x1 -> x2, starting transfers between devices: 3.72 us -> 8.18 us  [exchange(): return lax.all_to_all(value, axes, split_axis=0, concat_axis=0, tiled=True)]
    ppermute x2 -> x1, starting transfers between devices: 6.5 us -> 2.68 us  [with_halo(): lax.ppermute(head, axis, [((i + 1) % count, i) for i in range(count)])]
    all_to_all x1 -> x2, waiting for transfers between devices: 20.4 us -> 22.6 us  [exchange(): return lax.all_to_all(value, axes, split_axis=0, concat_axis=0, tiled=True)]
  transfers between devices with their start and end apart: 12 -> 8, of which waited for: 5 -> 6; matrix products, arithmetic and copies ran while one was open for 1% -> 2% of each run, Pallas kernels for 0% -> 0%
where the time goes in v2:
time: 223 us; the launch traced here: 222 us
  blocking collectives  118 us (53%)
  Pallas kernels  43.5 us (20%)
  waiting for transfers between devices  28.5 us (13%)
  starting transfers between devices  17.5 us (8%)
  local copies, waits for them, and re-layouts  5.71 us (3%)
  other arithmetic  5.39 us (2%)
  between operations  3.24 us (1%)
    all_to_all x3, blocking collectives, exchange(): return lax.all_to_all(value, axes, split_axis=0, concat_axis=0, tiled=True)  102 us
    all_to_all x2, waiting for transfers between devices, exchange(): return lax.all_to_all(value, axes, split_axis=0, concat_axis=0, tiled=True)  22.6 us
    pallas_call x1, Pallas kernels, body(): call(thetas, (1, qpoints, plane, part_z), [vmem] * 4, [pltpu.VMEM((qpoint...  18.3 us
    all_gather x1, blocking collectives, body(): lines = lax.all_gather(lines, 'gy', axis=1, tiled=True)  16.2 us
    pallas_call x1, Pallas kernels, body(): call(product_kernel, spectra.shape, [smem, smem, vmem, vmem, vmem, vmem],...  10.3 us
    all_to_all x2, starting transfers between devices, exchange(): return lax.all_to_all(value, axes, split_axis=0, concat_axis=0, tiled=True)  8.18 us
    ppermute x4, starting transfers between devices, global_max(): lax.ppermute(value, axis, [(i, (i + step) % count) for i in range(count)])  6.57 us
    pallas_call x1, Pallas kernels, body(): call(inverse_z_kernel, (groups_z, qpoints, rows, size_z), [vmem] * 3)  5.86 us
  transfers between devices with their start and end apart: 8, of which 6 were waited for; matrix products, arithmetic and copies ran while one was open for 2% of the time, Pallas kernels for 0%

profile of v2, /device:TPU:0, one launch (start us, length us, event | category | flops | bytes accessed | tf_op | source)
XLA Modules:
  0.0 221.8 jit_solution(13689038384338908056)
XLA Ops:
  0.0 4.3 %all-to-all-start = ((f32[4,4,16,128]{3,2,1,0:T(8,128)}), f32[4,4,16,128]{3,2,1,0:T(8,128)S(1)}, u32[]{:S(2)}, u32[]{:S(2)}) async-start(f32[4,4,16,128]{3,2,1,0:T(8,128)} %bitcast.20), calls=%async_computation | async-start | bytes 262144 | tf_op jit(solution)/shard_map/all_to_all | solution.py:205
  4.3 1.7 constant_dynamic-slice_fusion
  6.0 2.9 %all-to-all-done = f32[4,4,16,128]{3,2,1,0:T(8,128)S(1)} async-done(((f32[4,4,16,128]{3,2,1,0:T(8,128)}), f32[4,4,16,128]{3,2,1,0:T(8,128)S(1)}, u32[]{:S(2)}, u32[]{:S(2)}) %all-to-all-start) | async-done | bytes 131104 | tf_op jit(solution)/shard_map/all_to_all | solution.py:205
  8.9 16.2 %all_gather.3 = f32[4,64,512]{2,1,0:T(8,128)S(1)} all-gather(f32[4,16,512]{2,1,0:T(8,128)S(1)} %copy_bitcast_fusion), channel_id=1, replica_groups=mesh['gx'=2,'gy'=4,'gz'=4] {'gy'}, dimensions={1}, use_global_device_ids=true | all-gather | bytes 655360 | tf_op jit(solution)/shard_map/all_gather | solution.py:221
  25.0 0.0 copy-start
  25.1 0.1 collective-permute-start.1
  25.2 0.1 fusion.56
  25.3 2.7 %collective-permute-start = (f32[2,64,512]{2,1,0:T(8,128)S(1)}, f32[2,64,512]{2,1,0:T(8,128)S(1)}, u32[]{:S(2)}, u32[]{:S(2)}) collective-permute-start(f32[2,64,512]{2,1,0:T(8,128)S(1)} %get-tuple-element.7), channel_id=1, source_target_pairs={{1,0},{2,1},{3,2},{16,3},{17,16},{18,17},{19,18},{0,19},{5,4},{6,5... | collective-permute-start | bytes 786440 | tf_op jit(solution)/shard_map/ppermute | solution.py:78
  28.0 4.0 %collective-permute-done.1 = f32[2,64,512]{2,1,0:T(8,128)S(1)} collective-permute-done((f32[2,64,512]{2,1,0:T(8,128)S(1)}, f32[2,64,512]{2,1,0:T(8,128)S(1)}, u32[]{:S(2)}, u32[]{:S(2)}) %collective-permute-start.1) | collective-permute-done | bytes 262176 | tf_op jit(solution)/shard_map/ppermute | solution.py:77
  32.0 0.1 constant_dynamic-update-slice_fusion.1
  32.1 0.0 collective-permute-done
  32.1 0.0 copy-done
  32.1 2.7 %fusion.52 = (f32[]{:T(128)}, f32[4,64,512]{2,1,0:T(8,128)S(1)}) fusion(f32[4,64,512]{2,1,0:T(8,128)S(1)} %all_gather.3, f32[4,64,2]{2,1,0:T(8,128)S(1)} %get-tuple-element.14, f32[4,64,2]{2,1,0:T(8,128)S(1)} %get-tuple-element.13, f32[4,2,512]{2,1,0:T(2,128)S(1)} %get-tuple-element.12, f32[4,2,512]{2,1,0:T(2,128)S(1)} %get-tuple-element.11, ...), kind=kLoop, calls=%fused_computation.82 | loop fusion | flops 9830399 | bytes 3182596 | tf_op jit(solution)/shard_map/reduce_max | solution.py:228
  34.8 2.4 %collective-permute-start.2 = (f32[1,1]{1,0:T(1,128)}, f32[1,1]{1,0:T(1,128)}, u32[]{:S(2)}, u32[]{:S(2)}) collective-permute-start(f32[1,1]{1,0:T(1,128)} %bitcast.2), channel_id=1, source_target_pairs={{0,1},{1,2},{2,3},{3,0},{4,5},{5,6},{6,7},{7,4},{8,9},{9,10},{10,1... | collective-permute-start | bytes 20 | tf_op jit(solution)/shard_map/ppermute | solution.py:96
  37.1 0.6 collective-permute-start.3
  37.7 0.8 collective-permute-start.4
  38.5 0.3 collective-permute-done.2
  40.1 0.7 collective-permute-done.3
  41.4 0.0 collective-permute-done.4
  42.0 2.9 %collective-permute-start.5 = (f32[1,1]{1,0:T(1,128)}, f32[1,1]{1,0:T(1,128)}, u32[]{:S(2)}, u32[]{:S(2)}) collective-permute-start(f32[1,1]{1,0:T(1,128)} %max.20), channel_id=1, source_target_pairs={{0,16},{16,0},{1,17},{17,1},{2,18},{18,2},{3,19},{19,3},{4,20},{20... | collective-permute-start | bytes 20 | tf_op jit(solution)/shard_map/ppermute | solution.py:96
  44.9 0.9 collective-permute-done.5
  46.4 0.9 add_maximum_fusion
  47.3 18.3 %shard_map.154.in_ref = f32[1,14,256,128]{3,2,1,0:T(8,128)} custom-call(f32[256,512]{1,0:T(8,128)} %bitcast.17, f32[256,512]{1,0:T(8,128)} %bitcast.19, bf16[512,128]{1,0:T(8,128)(2,1)} %get-tuple-element.16.refs_2_, bf16[512,128]{1,0:T(8,128)(2,1)} %get-tuple-element.15.refs_3_), custom_call_target="tpu_custom_call" | custom-call | tf_op jit(solution)/shard_map/pallas_call | solution.py:241
  65.6 4.5 %shard_map.155 = f32[8,14,32,128]{3,2,1,0:T(8,128)} custom-call(bf16[256,256]{1,0:T(8,128)(2,1)} %constant.109.clone.high_ref, bf16[256,256]{1,0:T(8,128)(2,1)} %constant.110.clone.low_ref, f32[1,14,256,128]{3,2,1,0:T(8,128)} %shard_map.154.in_ref), custom_call_target="tpu_custom_call" | custom-call | tf_op jit(solution)/shard_map/pallas_call | solution.py:254
  70.1 0.0 copy-start.5
  70.1 0.0 copy-start.3
  70.1 3.9 %all-to-all-start.1 = ((f32[8,14,32,128]{3,2,1,0:T(8,128)}), f32[8,14,32,128]{3,2,1,0:T(8,128)S(1)}, u32[]{:S(2)}, u32[]{:S(2)}) async-start(f32[8,14,32,128]{3,2,1,0:T(8,128)} %shard_map.155), calls=%async_computation.1 | async-start | bytes 3670016 | tf_op jit(solution)/shard_map/all_to_all | solution.py:205
  74.1 0.0 copy-done.5
  74.1 0.1 dynamic_slice.12
  74.2 0.1 add.114
  74.2 0.0 copy-done.3
  74.3 0.1 add.109
  74.3 0.1 add.110
  74.4 0.8 dynamic_slice.13
  75.2 0.0 copy-done.2
  75.2 0.6 broadcast_multiply_fusion.coup_ref
  75.8 0.7 broadcast_add_fusion.wave_ref
  76.5 0.0 copy-done.4
  76.5 0.5 broadcast_multiply_fusion.1.mass_ref
  77.0 19.7 %all-to-all-done.1.in_ref = f32[8,14,32,128]{3,2,1,0:T(8,128)S(1)} async-done(((f32[8,14,32,128]{3,2,1,0:T(8,128)}), f32[8,14,32,128]{3,2,1,0:T(8,128)S(1)}, u32[]{:S(2)}, u32[]{:S(2)}) %all-to-all-start.1) | async-done | bytes 1835040 | tf_op jit(solution)/shard_map/all_to_all | solution.py:205
  96.7 1.2 copy-done.1
  97.9 10.3 %shard_map.156 = f32[8,14,32,128]{3,2,1,0:T(8,128)} custom-call(f32[14,14]{1,0:T(8,128)} %broadcast_multiply_fusion.coup_ref, f32[27]{0:T(128)} %broadcast_multiply_fusion.1.mass_ref, bf16[256,256]{1,0:T(8,128)(2,1)} %constant.115.clone.high_ref, bf16[256,256]{1,0:T(8,128)(2,1)} %constant.116.clone.low_ref, f32[256,128]{1,0:T(8,128)} %broadcast_add_fusion.wave_ref, ...), custom_call_target="tpu_custom_call" | custom-call | tf_op jit(solution)/shard_map/pallas_call | solution.py:265
  108.3 27.5 %all_to_all.25.in_ref = f32[8,14,32,128]{3,2,1,0:T(8,128)} all-to-all(f32[8,14,32,128]{3,2,1,0:T(8,128)} %shard_map.156), channel_id=1, replica_groups=mesh['gx'=2,'gy'=4,'gz'=4] {'gx','gz'}, dimensions={0} | all-to-all | bytes 3670016 | tf_op jit(solution)/shard_map/all_to_all | solution.py:205
  135.8 4.5 %shard_map.157 = f32[4,14,64,128]{3,2,1,0:T(8,128)} custom-call(bf16[256,256]{1,0:T(8,128)(2,1)} %constant.117.clone.high_ref, bf16[256,256]{1,0:T(8,128)(2,1)} %constant.118.clone.low_ref, f32[8,14,32,128]{3,2,1,0:T(8,128)} %all_to_all.25.in_ref), custom_call_target="tpu_custom_call" | custom-call | tf_op jit(solution)/shard_map/pallas_call | solution.py:273
  140.2 47.9 %all_to_all.26.in_ref = f32[4,14,64,128]{3,2,1,0:T(8,128)} all-to-all(f32[4,14,64,128]{3,2,1,0:T(8,128)} %shard_map.157), channel_id=1, replica_groups=mesh['gx'=2,'gy'=4,'gz'=4] {'gy'}, dimensions={0} | all-to-all | bytes 3670016 | tf_op jit(solution)/shard_map/all_to_all | solution.py:205
  188.1 5.9 %shard_map.158 = f32[4,14,64,128]{3,2,1,0:T(8,128)} custom-call(bf16[512,512]{1,0:T(8,128)(2,1)} %constant.107.clone.high_ref, bf16[512,512]{1,0:T(8,128)(2,1)} %constant.108.clone.low_ref, f32[4,14,64,128]{3,2,1,0:T(8,128)} %all_to_all.26.in_ref), custom_call_target="tpu_custom_call" | custom-call | tf_op jit(solution)/shard_map/pallas_call | solution.py:275
  194.0 26.4 %all_to_all.27 = f32[4,14,64,128]{3,2,1,0:T(8,128)S(1)} all-to-all(f32[4,14,64,128]{3,2,1,0:T(8,128)} %shard_map.158), channel_id=1, replica_groups=mesh['gx'=2,'gy'=4,'gz'=4] {'gz'}, dimensions={0} | all-to-all | bytes 3670016 | tf_op jit(solution)/shard_map/all_to_all | solution.py:205
  220.4 1.3 copy.20
  (10 shorter events, 0.1 us)
Async XLA Ops:
  0.0 8.9 %all-to-all-start = ((f32[4,4,16,128]{3,2,1,0:T(8,128)}), f32[4,4,16,128]{3,2,1,0:T(8,128)S(1)}, u32[]{:S(2)}, u32[]{:S(2)}) async-start(f32[4,4,16,128]{3,2,1,0:T(8,128)} %bitcast.20), calls=%async_computation | async-start | bytes 262144 | tf_op jit(solution)/shard_map/all_to_all | solution.py:205
  25.0 7.1 %copy-start = (f32[4,64,512]{2,1,0:T(8,128)}, f32[4,64,512]{2,1,0:T(8,128)S(1)}, u32[]{:S(2)}) copy-start(f32[4,64,512]{2,1,0:T(8,128)S(1)} %all_gather.3) | copy-start | bytes 1572868
  25.1 6.8 %collective-permute-start.1 = (f32[2,64,512]{2,1,0:T(8,128)S(1)}, f32[2,64,512]{2,1,0:T(8,128)S(1)}, u32[]{:S(2)}, u32[]{:S(2)}) collective-permute-start(f32[2,64,512]{2,1,0:T(8,128)S(1)} %get-tuple-element.8), channel_id=1, source_target_pairs={{0,1},{1,2},{2,3},{3,16},{16,17},{17,18},{18,19},{19,0},{4,5},{5,6... | collective-permute-start | bytes 786440 | tf_op jit(solution)/shard_map/ppermute | solution.py:77
  25.3 6.8 %collective-permute-start = (f32[2,64,512]{2,1,0:T(8,128)S(1)}, f32[2,64,512]{2,1,0:T(8,128)S(1)}, u32[]{:S(2)}, u32[]{:S(2)}) collective-permute-start(f32[2,64,512]{2,1,0:T(8,128)S(1)} %get-tuple-element.7), channel_id=1, source_target_pairs={{1,0},{2,1},{3,2},{16,3},{17,16},{18,17},{19,18},{0,19},{5,4},{6,5... | collective-permute-start | bytes 786440 | tf_op jit(solution)/shard_map/ppermute | solution.py:78
  34.8 4.0 %collective-permute-start.2 = (f32[1,1]{1,0:T(1,128)}, f32[1,1]{1,0:T(1,128)}, u32[]{:S(2)}, u32[]{:S(2)}) collective-permute-start(f32[1,1]{1,0:T(1,128)} %bitcast.2), channel_id=1, source_target_pairs={{0,1},{1,2},{2,3},{3,0},{4,5},{5,6},{6,7},{7,4},{8,9},{9,10},{10,1... | collective-permute-start | bytes 20 | tf_op jit(solution)/shard_map/ppermute | solution.py:96
  37.1 3.7 %collective-permute-start.3 = (f32[1,1]{1,0:T(1,128)}, f32[1,1]{1,0:T(1,128)}, u32[]{:S(2)}, u32[]{:S(2)}) collective-permute-start(f32[1,1]{1,0:T(1,128)} %bitcast.2), channel_id=1, source_target_pairs={{0,2},{1,3},{2,0},{3,1},{4,6},{5,7},{6,4},{7,5},{8,10},{9,11},{10,... | collective-permute-start | bytes 20 | tf_op jit(solution)/shard_map/ppermute | solution.py:96
  37.7 3.7 %collective-permute-start.4 = (f32[1,1]{1,0:T(1,128)}, f32[1,1]{1,0:T(1,128)}, u32[]{:S(2)}, u32[]{:S(2)}) collective-permute-start(f32[1,1]{1,0:T(1,128)} %bitcast.2), channel_id=1, source_target_pairs={{0,3},{1,0},{2,1},{3,2},{4,7},{5,4},{6,5},{7,6},{8,11},{9,8},{10,9... | collective-permute-start | bytes 20 | tf_op jit(solution)/shard_map/ppermute | solution.py:96
  42.0 3.7 %collective-permute-start.5 = (f32[1,1]{1,0:T(1,128)}, f32[1,1]{1,0:T(1,128)}, u32[]{:S(2)}, u32[]{:S(2)}) collective-permute-start(f32[1,1]{1,0:T(1,128)} %max.20), channel_id=1, source_target_pairs={{0,16},{16,0},{1,17},{17,1},{2,18},{18,2},{3,19},{19,3},{4,20},{20... | collective-permute-start | bytes 20 | tf_op jit(solution)/shard_map/ppermute | solution.py:96
  70.1 3.9 %copy-start.5 = (f32[64]{0:T(128)S(1)}, f32[64]{0:T(128)}, u32[]{:S(2)}) copy-start(f32[64]{0:T(128)} %constant.111.clone) | copy-start | bytes 772
  70.1 4.1 %copy-start.3 = (f32[32]{0:T(128)S(1)}, f32[32]{0:T(128)}, u32[]{:S(2)}) copy-start(f32[32]{0:T(128)} %constant.113.clone) | copy-start | bytes 388
  70.1 5.1 %copy-start.2 = (f32[14,14]{1,0:T(8,128)S(1)}, f32[14,14]{1,0:T(8,128)}, u32[]{:S(2)}) copy-start(f32[14,14]{1,0:T(8,128)} %param.17) | copy-start | bytes 2356
  70.1 6.4 %copy-start.4 = (f32[27]{0:T(128)S(1)}, f32[27]{0:T(128)}, u32[]{:S(2)}) copy-start(f32[27]{0:T(128)} %constant.114.clone) | copy-start | bytes 328
  70.1 26.6 %all-to-all-start.1 = ((f32[8,14,32,128]{3,2,1,0:T(8,128)}), f32[8,14,32,128]{3,2,1,0:T(8,128)S(1)}, u32[]{:S(2)}, u32[]{:S(2)}) async-start(f32[8,14,32,128]{3,2,1,0:T(8,128)} %shard_map.155), calls=%async_computation.1 | async-start | bytes 3670016 | tf_op jit(solution)/shard_map/all_to_all | solution.py:205
  96.7 1.2 copy-start.1

commit v3 on v2

--- a/solution.py
+++ b/solution.py
@@ -197,6 +197,7 @@
         in_specs=[pl.BlockSpec(memory_space=space) for space in specs],
         out_specs=pl.BlockSpec(memory_space=pltpu.VMEM),
         scratch_shapes=list(scratch),
+        cost_estimate=pl.CostEstimate(flops=2_000_000_000, bytes_accessed=4_000_000, transcendentals=0),
         compiler_params=pltpu.CompilerParams(vmem_limit_bytes=vmem_bytes),
     )
 
@@ -268,14 +269,19 @@
         [smem, smem, vmem, vmem, vmem, vmem],
         [pltpu.VMEM((qpoints, groups_xz * short, part_z), jnp.float32)],
     )(coupling / (full_x * full_y * full_z), masses, *split_table(x_matrix), waves, spectra)
-    returned = exchange(products, ("gx", "gz"))
-
-    fields = call(line_kernel, (groups_y, qpoints, rows, part_z), [vmem] * 3)(*split_table(y_matrix.T), returned)
-    fields = exchange(fields, "gy")
-    fields = call(inverse_z_kernel, (groups_z, qpoints, rows, size_z), [vmem] * 3)(*split_table(z_table), fields)
-    blocks = exchange(fields, "gz")
-    blocks = blocks.reshape(groups_z, qpoints, slab, size_y, size_z)
-    return blocks.transpose(1, 0, 2, 3, 4).reshape(qpoints, size_x, size_y, size_z)
+    y_back = split_table(y_matrix.T)
+    z_back = split_table(z_table)
+    middle = qpoints // 4 * 2
+    pieces = []
+    for part in (products[:, :middle], products[:, middle:]):
+        count = part.shape[1]
+        part = exchange(part, ("gx", "gz"))
+        part = call(line_kernel, (groups_y, count, rows, part_z), [vmem] * 3)(*y_back, part)
+        part = exchange(part, "gy")
+        part = call(inverse_z_kernel, (groups_z, count, rows, size_z), [vmem] * 3)(*z_back, part)
+        part = exchange(part, "gz").reshape(groups_z, count, slab, size_y, size_z)
+        pieces.append(part.transpose(1, 0, 2, 3, 4).reshape(count, size_x, size_y, size_z))
+    return jnp.concatenate(pieces, axis=0)
 
 
 def solution(mesh):

time: 223 us -> 236 us (1.058)
  blocking collectives: 118 us -> 16.2 us
  waiting for transfers between devices: 28.5 us -> 112 us
  starting transfers between devices: 17.5 us -> 40.8 us
  Pallas kernels: 43.5 us -> 47.2 us
    all_to_all x3 -> x0, blocking collectives: 102 us -> none  [exchange(): return lax.all_to_all(value, axes, split_axis=0, concat_axis=0, tiled=True)]
    all_to_all x2 -> x8, waiting for transfers between devices: 22.6 us -> 104 us  [exchange(): return lax.all_to_all(value, axes, split_axis=0, concat_axis=0, tiled=True)]
    all_to_all x2 -> x8, starting transfers between devices: 8.18 us -> 31.2 us  [exchange(): return lax.all_to_all(value, axes, split_axis=0, concat_axis=0, tiled=True)]
    pallas_call x2 -> x4, Pallas kernels: 10.3 us -> 14 us  [the longest x2 7.77 us: body(): call(inverse_z_kernel, (groups_z, count, rows, size_z), [vmem] * 3)]
    slice x0 -> x2, local copies, waits for them, and re-layouts: none -> 3.29 us  [the longest x1 2.2 us: body(): products[:, :middle]]
  transfers between devices with their start and end apart: 8 -> 14, of which waited for: 6 -> 11; matrix products, arithmetic and copies ran while one was open for 2% -> 3% of each run, Pallas kernels for 0% -> 6%
where the time goes in v3:
time: 236 us; the launch traced here: 235 us
  waiting for transfers between devices  112 us (47%)
  Pallas kernels  47.2 us (20%)
  starting transfers between devices  40.8 us (17%)
  blocking collectives  16.2 us (7%)
  local copies, waits for them, and re-layouts  7.78 us (3%)
  other arithmetic  6.82 us (3%)
  between operations  3.51 us (1%)
    all_to_all x8, waiting for transfers between devices, exchange(): return lax.all_to_all(value, axes, split_axis=0, concat_axis=0, tiled=True)  104 us
    all_to_all x8, starting transfers between devices, exchange(): return lax.all_to_all(value, axes, split_axis=0, concat_axis=0, tiled=True)  31.2 us
    pallas_call x1, Pallas kernels, body(): call(thetas, (1, qpoints, plane, part_z), [vmem] * 4, [pltpu.VMEM((qpoint...  18.3 us
    all_gather x1, blocking collectives, body(): lines = lax.all_gather(lines, 'gy', axis=1, tiled=True)  16.2 us
    pallas_call x1, Pallas kernels, body(): call(product_kernel, spectra.shape, [smem, smem, vmem, vmem, vmem, vmem],...  10.3 us
    pallas_call x2, Pallas kernels, body(): call(inverse_z_kernel, (groups_z, count, rows, size_z), [vmem] * 3)  7.77 us
    ppermute x4, starting transfers between devices, global_max(): lax.ppermute(value, axis, [(i, (i + step) % count) for i in range(count)])  6.85 us
    pallas_call x2, Pallas kernels, body(): call(line_kernel, (groups_y, count, rows, part_z), [vmem] * 3)  6.27 us
  transfers between devices with their start and end apart: 14, of which 11 were waited for; matrix products, arithmetic and copies ran while one was open for 3% of the time, Pallas kernels for 6%

profile of v3, /device:TPU:0, one launch (start us, length us, event | category | flops | bytes accessed | tf_op | source)
XLA Modules:
  0.0 234.6 jit_solution(13696569109431462058)
XLA Ops:
  0.0 4.3 %all-to-all-start = ((f32[4,4,16,128]{3,2,1,0:T(8,128)}), f32[4,4,16,128]{3,2,1,0:T(8,128)S(1)}, u32[]{:S(2)}, u32[]{:S(2)}) async-start(f32[4,4,16,128]{3,2,1,0:T(8,128)} %bitcast.27), calls=%async_computation | async-start | bytes 262144 | tf_op jit(solution)/shard_map/all_to_all | solution.py:206
  4.3 1.7 constant_dynamic-slice_fusion
  6.0 2.9 %all-to-all-done = f32[4,4,16,128]{3,2,1,0:T(8,128)S(1)} async-done(((f32[4,4,16,128]{3,2,1,0:T(8,128)}), f32[4,4,16,128]{3,2,1,0:T(8,128)S(1)}, u32[]{:S(2)}, u32[]{:S(2)}) %all-to-all-start) | async-done | bytes 131104 | tf_op jit(solution)/shard_map/all_to_all | solution.py:206
  8.9 16.2 %all_gather.3 = f32[4,64,512]{2,1,0:T(8,128)S(1)} all-gather(f32[4,16,512]{2,1,0:T(8,128)S(1)} %copy_bitcast_fusion), channel_id=1, replica_groups=mesh['gx'=2,'gy'=4,'gz'=4] {'gy'}, dimensions={1}, use_global_device_ids=true | all-gather | bytes 655360 | tf_op jit(solution)/shard_map/all_gather | solution.py:222
  25.2 0.1 fusion.56
  25.3 2.7 %collective-permute-start = (f32[2,64,512]{2,1,0:T(8,128)S(1)}, f32[2,64,512]{2,1,0:T(8,128)S(1)}, u32[]{:S(2)}, u32[]{:S(2)}) collective-permute-start(f32[2,64,512]{2,1,0:T(8,128)S(1)} %get-tuple-element.7), channel_id=1, source_target_pairs={{1,0},{2,1},{3,2},{16,3},{17,16},{18,17},{19,18},{0,19},{5,4},{6,5... | collective-permute-start | bytes 786440 | tf_op jit(solution)/shard_map/ppermute | solution.py:78
  28.0 4.0 %collective-permute-done.1 = f32[2,64,512]{2,1,0:T(8,128)S(1)} collective-permute-done((f32[2,64,512]{2,1,0:T(8,128)S(1)}, f32[2,64,512]{2,1,0:T(8,128)S(1)}, u32[]{:S(2)}, u32[]{:S(2)}) %collective-permute-start.1) | collective-permute-done | bytes 262176 | tf_op jit(solution)/shard_map/ppermute | solution.py:77
  32.0 0.1 constant_dynamic-update-slice_fusion.1
  32.1 2.7 %fusion.52 = (f32[]{:T(128)}, f32[4,64,512]{2,1,0:T(8,128)S(1)}) fusion(f32[4,64,512]{2,1,0:T(8,128)S(1)} %all_gather.3, f32[4,64,2]{2,1,0:T(8,128)S(1)} %get-tuple-element.14, f32[4,64,2]{2,1,0:T(8,128)S(1)} %get-tuple-element.13, f32[4,2,512]{2,1,0:T(2,128)S(1)} %get-tuple-element.12, f32[4,2,512]{2,1,0:T(2,128)S(1)} %get-tuple-element.11, ...), kind=kLoop, calls=%fused_computation.83 | loop fusion | flops 9830399 | bytes 3182596 | tf_op jit(solution)/shard_map/reduce_max | solution.py:229
  34.8 2.6 %collective-permute-start.4 = (f32[1,1]{1,0:T(1,128)}, f32[1,1]{1,0:T(1,128)}, u32[]{:S(2)}, u32[]{:S(2)}) collective-permute-start(f32[1,1]{1,0:T(1,128)} %bitcast.2), channel_id=1, source_target_pairs={{0,3},{1,0},{2,1},{3,2},{4,7},{5,4},{6,5},{7,6},{8,11},{9,8},{10,9... | collective-permute-start | bytes 20 | tf_op jit(solution)/shard_map/ppermute | solution.py:96
  37.3 1.4 collective-permute-start.3
  38.8 3.2 %collective-permute-done.2 = f32[1,1]{1,0:T(1,128)} collective-permute-done((f32[1,1]{1,0:T(1,128)}, f32[1,1]{1,0:T(1,128)}, u32[]{:S(2)}, u32[]{:S(2)}) %collective-permute-start.2) | collective-permute-done | bytes 36 | tf_op jit(solution)/shard_map/ppermute | solution.py:96
  44.6 2.9 %collective-permute-start.5 = (f32[1,1]{1,0:T(1,128)}, f32[1,1]{1,0:T(1,128)}, u32[]{:S(2)}, u32[]{:S(2)}) collective-permute-start(f32[1,1]{1,0:T(1,128)} %max.20), channel_id=1, source_target_pairs={{0,16},{16,0},{1,17},{17,1},{2,18},{18,2},{3,19},{19,3},{4,20},{20... | collective-permute-start | bytes 20 | tf_op jit(solution)/shard_map/ppermute | solution.py:96
  47.5 0.7 collective-permute-done.5
  48.9 0.9 add_maximum_fusion
  49.8 18.3 %shard_map.154.in_ref = f32[1,14,256,128]{3,2,1,0:T(8,128)} custom-call(f32[256,512]{1,0:T(8,128)} %bitcast.21, f32[256,512]{1,0:T(8,128)} %bitcast.26, bf16[512,128]{1,0:T(8,128)(2,1)} %get-tuple-element.16.refs_2_, bf16[512,128]{1,0:T(8,128)(2,1)} %get-tuple-element.15.refs_3_), custom_call_target="tpu_custom_call" | custom-call | flops 2000000000 | bytes 4000000 | tf_op jit(solution)/shard_map/pallas_call | solution.py:242
  68.1 4.5 %shard_map.155 = f32[8,14,32,128]{3,2,1,0:T(8,128)} custom-call(bf16[256,256]{1,0:T(8,128)(2,1)} %constant.109.clone.high_ref, bf16[256,256]{1,0:T(8,128)(2,1)} %constant.110.clone.low_ref, f32[1,14,256,128]{3,2,1,0:T(8,128)} %shard_map.154.in_ref), custom_call_target="tpu_custom_call" | custom-call | flops 2000000000 | bytes 4000000 | tf_op jit(solution)/shard_map/pallas_call | solution.py:255
  72.7 3.9 %all-to-all-start.1 = ((f32[8,14,32,128]{3,2,1,0:T(8,128)}), f32[8,14,32,128]{3,2,1,0:T(8,128)S(1)}, u32[]{:S(2)}, u32[]{:S(2)}) async-start(f32[8,14,32,128]{3,2,1,0:T(8,128)} %shard_map.155), calls=%async_computation.1 | async-start | bytes 3670016 | tf_op jit(solution)/shard_map/all_to_all | solution.py:206
  76.6 0.8 dynamic_slice.13
  77.3 0.1 dynamic_slice.12
  77.4 0.1 add.114
  77.5 0.1 add.109
  77.6 0.1 add.110
  77.7 0.6 broadcast_multiply_fusion.coup_ref
  78.3 0.7 broadcast_add_fusion.wave_ref
  79.1 0.5 broadcast_multiply_fusion.1.mass_ref
  79.6 19.7 %all-to-all-done.1.in_ref = f32[8,14,32,128]{3,2,1,0:T(8,128)S(1)} async-done(((f32[8,14,32,128]{3,2,1,0:T(8,128)}), f32[8,14,32,128]{3,2,1,0:T(8,128)S(1)}, u32[]{:S(2)}, u32[]{:S(2)}) %all-to-all-start.1) | async-done | bytes 1835040 | tf_op jit(solution)/shard_map/all_to_all | solution.py:206
  99.2 1.2 copy-done.1
  100.5 10.3 %shard_map.156 = f32[8,14,32,128]{3,2,1,0:T(8,128)} custom-call(f32[14,14]{1,0:T(8,128)} %broadcast_multiply_fusion.coup_ref, f32[27]{0:T(128)} %broadcast_multiply_fusion.1.mass_ref, bf16[256,256]{1,0:T(8,128)(2,1)} %constant.115.clone.high_ref, bf16[256,256]{1,0:T(8,128)(2,1)} %constant.116.clone.low_ref, f32[256,128]{1,0:T(8,128)} %broadcast_add_fusion.wave_ref, ...), custom_call_target="tpu_custom_call" | custom-call | flops 2000000000 | bytes 4000000 | tf_op jit(solution)/shard_map/pallas_call | solution.py:266
  110.8 2.2 slice.110
  113.0 3.5 %all-to-all-start.2 = ((f32[8,6,32,128]{3,2,1,0:T(8,128)}), f32[8,6,32,128]{3,2,1,0:T(8,128)S(1)}, u32[]{:S(2)}, u32[]{:S(2)}) async-start(f32[8,6,32,128]{3,2,1,0:T(8,128)} %slice.110), calls=%async_computation.2 | async-start | bytes 1572864 | tf_op jit(solution)/shard_map/all_to_all | solution.py:206
  116.6 1.1 slice.111
  117.6 10.5 %all-to-all-done.2.in_ref = f32[8,6,32,128]{3,2,1,0:T(8,128)S(1)} async-done(((f32[8,6,32,128]{3,2,1,0:T(8,128)}), f32[8,6,32,128]{3,2,1,0:T(8,128)S(1)}, u32[]{:S(2)}, u32[]{:S(2)}) %all-to-all-start.2) | async-done | bytes 786464 | tf_op jit(solution)/shard_map/all_to_all | solution.py:206
  128.1 3.6 %all-to-all-start.5 = ((f32[8,8,32,128]{3,2,1,0:T(8,128)}), f32[8,8,32,128]{3,2,1,0:T(8,128)S(1)}, u32[]{:S(2)}, u32[]{:S(2)}) async-start(f32[8,8,32,128]{3,2,1,0:T(8,128)} %slice.111), calls=%async_computation.5 | async-start | bytes 2097152 | tf_op jit(solution)/shard_map/all_to_all | solution.py:206
  131.7 2.9 %shard_map.157 = f32[4,6,64,128]{3,2,1,0:T(8,128)} custom-call(bf16[256,256]{1,0:T(8,128)(2,1)} %constant.117.clone.high_ref, bf16[256,256]{1,0:T(8,128)(2,1)} %constant.118.clone.low_ref, f32[8,6,32,128]{3,2,1,0:T(8,128)} %copy-done.6), custom_call_target="tpu_custom_call" | custom-call | flops 2000000000 | bytes 4000000 | tf_op jit(solution)/shard_map/pallas_call | solution.py:279
  134.7 11.4 %all-to-all-done.5.in_ref = f32[8,8,32,128]{3,2,1,0:T(8,128)S(1)} async-done(((f32[8,8,32,128]{3,2,1,0:T(8,128)}), f32[8,8,32,128]{3,2,1,0:T(8,128)S(1)}, u32[]{:S(2)}, u32[]{:S(2)}) %all-to-all-start.5) | async-done | bytes 1048608 | tf_op jit(solution)/shard_map/all_to_all | solution.py:206
  146.1 5.4 %all-to-all-start.3 = ((f32[4,6,64,128]{3,2,1,0:T(8,128)}), f32[4,6,64,128]{3,2,1,0:T(8,128)S(1)}, u32[]{:S(2)}, u32[]{:S(2)}) async-start(f32[4,6,64,128]{3,2,1,0:T(8,128)} %shard_map.157), calls=%async_computation.3 | async-start | bytes 1572864 | tf_op jit(solution)/shard_map/all_to_all | solution.py:206
  151.5 3.3 %shard_map.159 = f32[4,8,64,128]{3,2,1,0:T(8,128)} custom-call(bf16[256,256]{1,0:T(8,128)(2,1)} %constant.117.clone.high_ref, bf16[256,256]{1,0:T(8,128)(2,1)} %constant.118.clone.low_ref, f32[8,8,32,128]{3,2,1,0:T(8,128)} %copy-done.3), custom_call_target="tpu_custom_call" | custom-call | flops 2000000000 | bytes 4000000 | tf_op jit(solution)/shard_map/pallas_call | solution.py:279
  154.8 16.5 %all-to-all-done.3.in_ref = f32[4,6,64,128]{3,2,1,0:T(8,128)S(1)} async-done(((f32[4,6,64,128]{3,2,1,0:T(8,128)}), f32[4,6,64,128]{3,2,1,0:T(8,128)S(1)}, u32[]{:S(2)}, u32[]{:S(2)}) %all-to-all-start.3) | async-done | bytes 786464 | tf_op jit(solution)/shard_map/all_to_all | solution.py:206
  171.3 3.5 %all-to-all-start.6 = ((f32[4,8,64,128]{3,2,1,0:T(8,128)}), f32[4,8,64,128]{3,2,1,0:T(8,128)S(1)}, u32[]{:S(2)}, u32[]{:S(2)}) async-start(f32[4,8,64,128]{3,2,1,0:T(8,128)} %shard_map.159), calls=%async_computation.6 | async-start | bytes 2097152 | tf_op jit(solution)/shard_map/all_to_all | solution.py:206
  174.9 3.6 %shard_map.158 = f32[4,6,64,128]{3,2,1,0:T(8,128)} custom-call(bf16[512,512]{1,0:T(8,128)(2,1)} %constant.107.clone.high_ref, bf16[512,512]{1,0:T(8,128)(2,1)} %constant.108.clone.low_ref, f32[4,6,64,128]{3,2,1,0:T(8,128)} %copy-done.5), custom_call_target="tpu_custom_call" | custom-call | flops 2000000000 | bytes 4000000 | tf_op jit(solution)/shard_map/pallas_call | solution.py:281
  178.5 21.6 %all-to-all-done.6.in_ref = f32[4,8,64,128]{3,2,1,0:T(8,128)S(1)} async-done(((f32[4,8,64,128]{3,2,1,0:T(8,128)}), f32[4,8,64,128]{3,2,1,0:T(8,128)S(1)}, u32[]{:S(2)}, u32[]{:S(2)}) %all-to-all-start.6) | async-done | bytes 1048608 | tf_op jit(solution)/shard_map/all_to_all | solution.py:206
  200.1 3.5 %all-to-all-start.4 = ((f32[4,6,64,128]{3,2,1,0:T(8,128)}), f32[4,6,64,128]{3,2,1,0:T(8,128)S(1)}, u32[]{:S(2)}, u32[]{:S(2)}) async-start(f32[4,6,64,128]{3,2,1,0:T(8,128)} %shard_map.158), calls=%async_computation.4 | async-start | bytes 1572864 | tf_op jit(solution)/shard_map/all_to_all | solution.py:206
  203.6 4.2 %shard_map.160 = f32[4,8,64,128]{3,2,1,0:T(8,128)} custom-call(bf16[512,512]{1,0:T(8,128)(2,1)} %constant.107.clone.high_ref, bf16[512,512]{1,0:T(8,128)(2,1)} %constant.108.clone.low_ref, f32[4,8,64,128]{3,2,1,0:T(8,128)} %copy-done.4), custom_call_target="tpu_custom_call" | custom-call | flops 2000000000 | bytes 4000000 | tf_op jit(solution)/shard_map/pallas_call | solution.py:281
  207.8 7.4 %all-to-all-done.4 = f32[4,6,64,128]{3,2,1,0:T(8,128)S(1)} async-done(((f32[4,6,64,128]{3,2,1,0:T(8,128)}), f32[4,6,64,128]{3,2,1,0:T(8,128)S(1)}, u32[]{:S(2)}, u32[]{:S(2)}) %all-to-all-start.4) | async-done | bytes 786464 | tf_op jit(solution)/shard_map/all_to_all | solution.py:206
  215.2 3.5 %all-to-all-start.7 = ((f32[4,8,64,128]{3,2,1,0:T(8,128)}), f32[4,8,64,128]{3,2,1,0:T(8,128)S(1)}, u32[]{:S(2)}, u32[]{:S(2)}) async-start(f32[4,8,64,128]{3,2,1,0:T(8,128)} %shard_map.160), calls=%async_computation.7 | async-start | bytes 2097152 | tf_op jit(solution)/shard_map/all_to_all | solution.py:206
  218.8 14.3 %all-to-all-done.7 = f32[4,8,64,128]{3,2,1,0:T(8,128)S(1)} async-done(((f32[4,8,64,128]{3,2,1,0:T(8,128)}), f32[4,8,64,128]{3,2,1,0:T(8,128)S(1)}, u32[]{:S(2)}, u32[]{:S(2)}) %all-to-all-start.7) | async-done | bytes 1048608 | tf_op jit(solution)/shard_map/all_to_all | solution.py:206
  233.2 1.4 pad_maximum_fusion
  (35 shorter events, 0.4 us)
Async XLA Ops:
  0.0 8.9 %all-to-all-start = ((f32[4,4,16,128]{3,2,1,0:T(8,128)}), f32[4,4,16,128]{3,2,1,0:T(8,128)S(1)}, u32[]{:S(2)}, u32[]{:S(2)}) async-start(f32[4,4,16,128]{3,2,1,0:T(8,128)} %bitcast.27), calls=%async_computation | async-start | bytes 262144 | tf_op jit(solution)/shard_map/all_to_all | solution.py:206
  25.0 7.1 %copy-start = (f32[4,64,512]{2,1,0:T(8,128)}, f32[4,64,512]{2,1,0:T(8,128)S(1)}, u32[]{:S(2)}) copy-start(f32[4,64,512]{2,1,0:T(8,128)S(1)} %all_gather.3) | copy-start | bytes 1572868
  25.1 6.8 %collective-permute-start.1 = (f32[2,64,512]{2,1,0:T(8,128)S(1)}, f32[2,64,512]{2,1,0:T(8,128)S(1)}, u32[]{:S(2)}, u32[]{:S(2)}) collective-permute-start(f32[2,64,512]{2,1,0:T(8,128)S(1)} %get-tuple-element.8), channel_id=1, source_target_pairs={{0,1},{1,2},{2,3},{3,16},{16,17},{17,18},{18,19},{19,0},{4,5},{5,6... | collective-permute-start | bytes 786440 | tf_op jit(solution)/shard_map/ppermute | solution.py:77
  25.3 6.8 %collective-permute-start = (f32[2,64,512]{2,1,0:T(8,128)S(1)}, f32[2,64,512]{2,1,0:T(8,128)S(1)}, u32[]{:S(2)}, u32[]{:S(2)}) collective-permute-start(f32[2,64,512]{2,1,0:T(8,128)S(1)} %get-tuple-element.7), channel_id=1, source_target_pairs={{1,0},{2,1},{3,2},{16,3},{17,16},{18,17},{19,18},{0,19},{5,4},{6,5... | collective-permute-start | bytes 786440 | tf_op jit(solution)/shard_map/ppermute | solution.py:78
  34.8 9.1 %collective-permute-start.4 = (f32[1,1]{1,0:T(1,128)}, f32[1,1]{1,0:T(1,128)}, u32[]{:S(2)}, u32[]{:S(2)}) collective-permute-start(f32[1,1]{1,0:T(1,128)} %bitcast.2), channel_id=1, source_target_pairs={{0,3},{1,0},{2,1},{3,2},{4,7},{5,4},{6,5},{7,6},{8,11},{9,8},{10,9... | collective-permute-start | bytes 20 | tf_op jit(solution)/shard_map/ppermute | solution.py:96
  37.3 6.0 %collective-permute-start.3 = (f32[1,1]{1,0:T(1,128)}, f32[1,1]{1,0:T(1,128)}, u32[]{:S(2)}, u32[]{:S(2)}) collective-permute-start(f32[1,1]{1,0:T(1,128)} %bitcast.2), channel_id=1, source_target_pairs={{0,2},{1,3},{2,0},{3,1},{4,6},{5,7},{6,4},{7,5},{8,10},{9,11},{10,... | collective-permute-start | bytes 20 | tf_op jit(solution)/shard_map/ppermute | solution.py:96
  38.8 3.2 %collective-permute-start.2 = (f32[1,1]{1,0:T(1,128)}, f32[1,1]{1,0:T(1,128)}, u32[]{:S(2)}, u32[]{:S(2)}) collective-permute-start(f32[1,1]{1,0:T(1,128)} %bitcast.2), channel_id=1, source_target_pairs={{0,1},{1,2},{2,3},{3,0},{4,5},{5,6},{6,7},{7,4},{8,9},{9,10},{10,1... | collective-permute-start | bytes 20 | tf_op jit(solution)/shard_map/ppermute | solution.py:96
  44.6 3.6 %collective-permute-start.5 = (f32[1,1]{1,0:T(1,128)}, f32[1,1]{1,0:T(1,128)}, u32[]{:S(2)}, u32[]{:S(2)}) collective-permute-start(f32[1,1]{1,0:T(1,128)} %max.20), channel_id=1, source_target_pairs={{0,16},{16,0},{1,17},{17,1},{2,18},{18,2},{3,19},{19,3},{4,20},{20... | collective-permute-start | bytes 20 | tf_op jit(solution)/shard_map/ppermute | solution.py:96
  72.6 4.7 %copy-start.10 = (f32[64]{0:T(128)S(1)}, f32[64]{0:T(128)}, u32[]{:S(2)}) copy-start(f32[64]{0:T(128)} %constant.111.clone) | copy-start | bytes 772
  72.6 4.9 %copy-start.8 = (f32[32]{0:T(128)S(1)}, f32[32]{0:T(128)}, u32[]{:S(2)}) copy-start(f32[32]{0:T(128)} %constant.113.clone) | copy-start | bytes 388
  72.6 5.1 %copy-start.7 = (f32[14,14]{1,0:T(8,128)S(1)}, f32[14,14]{1,0:T(8,128)}, u32[]{:S(2)}) copy-start(f32[14,14]{1,0:T(8,128)} %param.17) | copy-start | bytes 2356
  72.6 6.4 %copy-start.9 = (f32[27]{0:T(128)S(1)}, f32[27]{0:T(128)}, u32[]{:S(2)}) copy-start(f32[27]{0:T(128)} %constant.114.clone) | copy-start | bytes 328
  72.7 26.6 %all-to-all-start.1 = ((f32[8,14,32,128]{3,2,1,0:T(8,128)}), f32[8,14,32,128]{3,2,1,0:T(8,128)S(1)}, u32[]{:S(2)}, u32[]{:S(2)}) async-start(f32[8,14,32,128]{3,2,1,0:T(8,128)} %shard_map.155), calls=%async_computation.1 | async-start | bytes 3670016 | tf_op jit(solution)/shard_map/all_to_all | solution.py:206
  99.2 1.2 copy-start.1
  110.8 5.8 %copy-start.2 = (f32[8,14,32,128]{3,2,1,0:T(8,128)S(1)}, f32[8,14,32,128]{3,2,1,0:T(8,128)}, u32[]{:S(2)}) copy-start(f32[8,14,32,128]{3,2,1,0:T(8,128)} %shard_map.156) | copy-start | bytes 5505028
  113.0 15.1 %all-to-all-start.2 = ((f32[8,6,32,128]{3,2,1,0:T(8,128)}), f32[8,6,32,128]{3,2,1,0:T(8,128)S(1)}, u32[]{:S(2)}, u32[]{:S(2)}) async-start(f32[8,6,32,128]{3,2,1,0:T(8,128)} %slice.110), calls=%async_computation.2 | async-start | bytes 1572864 | tf_op jit(solution)/shard_map/all_to_all | solution.py:206
  128.1 3.6 %copy-start.6 = (f32[8,6,32,128]{3,2,1,0:T(8,128)}, f32[8,6,32,128]{3,2,1,0:T(8,128)S(1)}, u32[]{:S(2)}) copy-start(f32[8,6,32,128]{3,2,1,0:T(8,128)S(1)} %all-to-all-done.2.in_ref) | copy-start | bytes 2359300
  128.1 18.0 %all-to-all-start.5 = ((f32[8,8,32,128]{3,2,1,0:T(8,128)}), f32[8,8,32,128]{3,2,1,0:T(8,128)S(1)}, u32[]{:S(2)}, u32[]{:S(2)}) async-start(f32[8,8,32,128]{3,2,1,0:T(8,128)} %slice.111), calls=%async_computation.5 | async-start | bytes 2097152 | tf_op jit(solution)/shard_map/all_to_all | solution.py:206
  146.1 5.4 %copy-start.3 = (f32[8,8,32,128]{3,2,1,0:T(8,128)}, f32[8,8,32,128]{3,2,1,0:T(8,128)S(1)}, u32[]{:S(2)}) copy-start(f32[8,8,32,128]{3,2,1,0:T(8,128)S(1)} %all-to-all-done.5.in_ref) | copy-start | bytes 3145732
  146.1 25.2 %all-to-all-start.3 = ((f32[4,6,64,128]{3,2,1,0:T(8,128)}), f32[4,6,64,128]{3,2,1,0:T(8,128)S(1)}, u32[]{:S(2)}, u32[]{:S(2)}) async-start(f32[4,6,64,128]{3,2,1,0:T(8,128)} %shard_map.157), calls=%async_computation.3 | async-start | bytes 1572864 | tf_op jit(solution)/shard_map/all_to_all | solution.py:206
  171.3 3.5 %copy-start.5 = (f32[4,6,64,128]{3,2,1,0:T(8,128)}, f32[4,6,64,128]{3,2,1,0:T(8,128)S(1)}, u32[]{:S(2)}) copy-start(f32[4,6,64,128]{3,2,1,0:T(8,128)S(1)} %all-to-all-done.3.in_ref) | copy-start | bytes 2359300
  171.3 28.8 %all-to-all-start.6 = ((f32[4,8,64,128]{3,2,1,0:T(8,128)}), f32[4,8,64,128]{3,2,1,0:T(8,128)S(1)}, u32[]{:S(2)}, u32[]{:S(2)}) async-start(f32[4,8,64,128]{3,2,1,0:T(8,128)} %shard_map.159), calls=%async_computation.6 | async-start | bytes 2097152 | tf_op jit(solution)/shard_map/all_to_all | solution.py:206
  200.1 3.5 %copy-start.4 = (f32[4,8,64,128]{3,2,1,0:T(8,128)}, f32[4,8,64,128]{3,2,1,0:T(8,128)S(1)}, u32[]{:S(2)}) copy-start(f32[4,8,64,128]{3,2,1,0:T(8,128)S(1)} %all-to-all-done.6.in_ref) | copy-start | bytes 3145732
  200.1 15.1 %all-to-all-start.4 = ((f32[4,6,64,128]{3,2,1,0:T(8,128)}), f32[4,6,64,128]{3,2,1,0:T(8,128)S(1)}, u32[]{:S(2)}, u32[]{:S(2)}) async-start(f32[4,6,64,128]{3,2,1,0:T(8,128)} %shard_map.158), calls=%async_computation.4 | async-start | bytes 1572864 | tf_op jit(solution)/shard_map/all_to_all | solution.py:206
  215.2 17.9 %all-to-all-start.7 = ((f32[4,8,64,128]{3,2,1,0:T(8,128)}), f32[4,8,64,128]{3,2,1,0:T(8,128)S(1)}, u32[]{:S(2)}, u32[]{:S(2)}) async-start(f32[4,8,64,128]{3,2,1,0:T(8,128)} %shard_map.160), calls=%async_computation.7 | async-start | bytes 2097152 | tf_op jit(solution)/shard_map/all_to_all | solution.py:206
